TPU v7x, 256 devices: a whole 4x4x8 slice. The times are simulated.
256 devices in a mesh: dp: 64 (over x, z, core), mp: 4 (over y).
Axes of the slice: x: 4, y: 4, z: 8, core: 2. Of those that a mesh axis runs over, the one named last changes fastest.
Arguments:
- gradients: bfloat16 [32, 2048, 4096], P(None, 'dp', 'mp'), may hold values from -6 to 6
- statistics: float32 [65536, 4096], P('dp', 'mp'), may hold values from -3 to 3300, as said below
- row_counts: int32 [64], replicated, may hold values from 1 to 32, 1024 in all
- block_pair: int32 [32], replicated, may hold values from 0 to 31, each once
Outputs:
- update: bfloat16 [32, 2048, 4096], P(None, 'dp', 'mp')
- new_statistics: float32 [65536, 4096], P('dp', 'mp')
Inputs may be any that keep to these rules, and one draw needn't show every extreme that they name: `row_counts`: the counts sum to 1024; the largest is exactly 32. `block_pair`: every pair index appears exactly once. `statistics`: each 1024 x 1024 block held by one device is symmetric positive definite.
All inputs are finite; a program needn't handle non-finite values. Where the computation divides by a largest or mean magnitude, that divisor is 1e-20 or more.
Results may differ from a plain program's by a relative error of at most 0.0078.
The roundings to bfloat16 on the way count: a program that leaves them out, or rounds other values in their place, can miss the bound.
Values may be sent and summed in bfloat16 or wider, within the bound.
A program may use at most 64 MiB of HBM per device.

v0:
```python
import functools

import jax
import jax.numpy as jnp
from jax import lax
from jax.sharding import Mesh
from jax.sharding import PartitionSpec as P

ITERS = 2
DP = ("dp_0", "dp_1", "dp_2")
DP_MP = ("dp_0", "dp_1", "dp_2", "mp")


decay_rate = 0.95
epsilon = 1e-06


def from_partner(array, axis, stride):
    return lax.ppermute(array, axis, [(i, i ^ 1 << stride) for i in range(lax.axis_size(axis))])


def by_axis(array, axes):
    return functools.reduce(lax.psum, axes, array)


def inverse_root(accumulated):
    block_size = accumulated.shape[0]
    bound = jnp.max(jnp.sum(jnp.abs(accumulated), axis=1))
    identity = jnp.eye(block_size, dtype=jnp.float32)
    moment = accumulated / bound
    factor = bound ** (-0.25)
    inv_root = None
    for iteration in range(ITERS):
        shifted = (5.0 * identity - moment) * 0.25
        poly_step = shifted.astype(jnp.bfloat16)
        if iteration == 0:
            inv_root = (factor * shifted).astype(jnp.bfloat16)
        else:
            inv_root = jnp.dot(inv_root, poly_step, preferred_element_type=jnp.float32).astype(
                jnp.bfloat16
            )
        if iteration + 1 < ITERS:
            square = jnp.dot(poly_step, poly_step, preferred_element_type=jnp.float32).astype(
                jnp.bfloat16
            )
            fourth = jnp.dot(square, square, preferred_element_type=jnp.float32).astype(
                jnp.bfloat16
            )
            moment = jnp.dot(
                fourth, moment.astype(jnp.bfloat16), preferred_element_type=jnp.float32
            )
    return inv_root


def body(gradients, statistics, row_counts, block_pair):
    blocks, slot_rows, block_size = gradients.shape
    devices = lax.axis_size(DP)
    strips = lax.axis_size("mp")
    position = lax.axis_index(DP)
    parity = position % 2
    pair_ids = jnp.arange(devices // 2, dtype=jnp.int32)
    block_ids = jnp.arange(blocks, dtype=jnp.int32)
    block_of_pair = jnp.sum(
        block_ids[None, :] * (block_pair[None, :] == pair_ids[:, None]).astype(jnp.int32), axis=1
    )
    peer_ids = jnp.arange(devices, dtype=jnp.int32)
    peer_block = block_of_pair[peer_ids // 2]
    peer_parity = peer_ids % 2
    offsets = jnp.cumsum(row_counts) - row_counts
    row_ids = jnp.arange(block_size, dtype=jnp.int32)
    source = jnp.sum((offsets[None, :] <= row_ids[:, None]).astype(jnp.int32), axis=1) - 1
    gather_rows = source * slot_rows + row_ids - offsets[source]
    halves = gradients.reshape(blocks, 2, slot_rows // 2, block_size)
    outgoing = halves[peer_block, peer_parity]
    own_half = lax.all_to_all(outgoing, DP, split_axis=0, concat_axis=0, tiled=True)
    other_half = from_partner(own_half, DP, 0)
    lower = jnp.where(parity == 0, own_half, other_half)
    upper = jnp.where(parity == 0, other_half, own_half)
    received = jnp.concatenate([lower, upper], axis=1)
    block_grad = jnp.take(received.reshape(devices * slot_rows, block_size), gather_rows, axis=0)
    oriented = jnp.where(parity == 0, block_grad, block_grad.T)
    gram = jnp.dot(oriented, oriented.T, preferred_element_type=jnp.float32)
    accumulated = decay_rate * statistics + (1.0 - decay_rate) * gram
    inv_root = inverse_root(accumulated)
    partner_root = from_partner(inv_root, DP, 0)
    left_root = jnp.where(parity == 0, inv_root, partner_root)
    right_root = jnp.where(parity == 0, partner_root, inv_root)
    entries = strips * blocks * block_size * block_size
    part_slots = slot_rows // 2
    slot_pos = parity * part_slots + jnp.arange(part_slots, dtype=jnp.int32)
    targets = offsets[:, None] + slot_pos[None, :]
    valid = slot_pos[None, :] < row_counts[:, None]
    picked = jnp.take(left_root, jnp.clip(targets, 0, block_size - 1).reshape(-1), axis=0)
    half_prod = jnp.dot(picked, block_grad, preferred_element_type=jnp.float32).astype(jnp.bfloat16)
    direction = jnp.dot(half_prod, right_root, preferred_element_type=jnp.float32)
    direction = jnp.where(valid.reshape(-1, 1), direction, 0.0)
    total_sum = by_axis(jnp.sum(direction * direction), DP_MP)
    inv_rms = lax.rsqrt(total_sum / entries + epsilon)
    scaled = (direction * inv_rms).astype(jnp.bfloat16)
    first_owner = 2 * block_pair
    outgoing_back = scaled.reshape(devices, part_slots, block_size)
    returned = lax.all_to_all(outgoing_back, DP, split_axis=0, concat_axis=0, tiled=True)
    update = jnp.concatenate([returned[first_owner], returned[first_owner + 1]], axis=1)
    return (update, accumulated)


def solution(mesh):
    torus = Mesh(mesh.devices.reshape(4, 8, 2, mesh.shape["mp"]), ("dp_0", "dp_1", "dp_2", "mp"))
    placed = (P(None, DP, "mp"), P(DP, "mp"), P(), P())
    return jax.shard_map(
        body,
        mesh=torus,
        in_specs=placed,
        out_specs=(P(None, DP, "mp"), P(DP, "mp")),
        check_vma=False,
    )
```

profile of v0, /device:TPU:1, one launch (start us, length us, event | category | flops | bytes accessed | tf_op | source)
XLA Modules:
  0.0 303.5 jit_solution(15443059343167768635)
XLA Ops:
  0.6 0.0 copy-start
  0.7 0.9 select_reduce_fusion
  1.6 0.8 gather_fusion
  2.4 0.0 copy-done
  2.4 2.0 gather_fusion.1
  4.4 64.3 %all_to_all.10 = bf16[64,16,1024]{2,1,0:T(8,128)(2,1)S(1)} all-to-all(bf16[64,16,1024]{2,1,0:T(8,128)(2,1)} %gather_fusion.1), channel_id=1, replica_groups=mesh['dp_0'=4,'dp_1'=8,'dp_2'=2,'mp'=4] {'dp_0','dp_1','dp_2'}, dimensions={0} | all-to-all | bytes 4194304 | tf_op jit(solution)/shard_map/all_to_all | solution.py:75
  68.7 0.4 collective-permute-start
  69.1 0.0 copy-done.6
  69.1 0.1 copy.21
  69.2 0.1 reduce-window.9
  69.3 0.1 reduce
  69.4 5.4 %copy.22 = f32[1024,1024]{0,1:T(8,128)} copy(f32[1024,1024]{1,0:T(8,128)} %param.5) | data formatting | bytes 8388608 | tf_op args[1]
  74.8 0.7 fusion.60
  75.5 0.7 fusion.57
  76.2 0.7 fusion.58
  76.9 0.7 fusion.59
  77.7 0.1 convert_reduce_fusion
  77.8 4.3 %compare_select_fusion.3 = (s32[1024,1]{0,1:T(1,128)S(1)}, s32[1024,1]{0,1:T(1,128)S(1)}) fusion(s32[]{:T(128)} %bitcast.60, s32[]{:T(128)} %bitcast.61, s32[]{:T(128)} %bitcast.62, s32[]{:T(128)} %bitcast.63, s32[]{:T(128)} %bitcast.64, s32[]{:T(128)} %bitcast.66, s32[]{:T(128)} %bitcast.65, s32[1024,1]{0,1:T(1,128)S(1)} %bitcast.96, s32[1024,1]{0,1:T(1,128)S(1)} %bitcast.92), kind=kLoop, calls=%fused_computation.115 | loop fusion | flops 14336 | bytes 16412 | tf_op jit(solution)/shard_map/gather | solution.py:72
  82.1 0.7 compare_reduce_fusion.56
  82.9 36.0 %compare_and_fusion = (pred[1024]{0:T(1024)(128)(4,1)S(1)}, s32[1024]{0:T(1024)S(1)}) fusion(s32[1024]{0:T(1024)S(1)} %convert_reduce_fusion, pred[1024]{0:T(1024)(128)(4,1)S(1)} %get-tuple-element.64, pred[1024]{0:T(1024)(128)(4,1)S(1)} %get-tuple-element.63, pred[1024]{0:T(1024)(128)(4,1)S(1)} %get-tuple-element.62, ...), kind=kLoop, calls=%fused_computation.127 | loop fusion | flops 68608 | bytes 71908 | tf_op jit(solution)/shard_map/jit(_take)/and | solution.py:80
  118.8 0.0 collective-permute-done
  118.9 1.9 broadcast_select_fusion.1
  120.7 2.8 pad_maximum_fusion
  123.6 7.7 %gather_fusion.2 = bf16[1024,1024]{1,0:T(8,128)(2,1)S(1)} fusion(bf16[2048,1024]{1,0:T(8,128)(2,1)} %bitcast.90, s32[1024]{0:T(1024)S(1)} %broadcast_clamp_fusion.1), kind=kCustom, calls=%fused_computation.2 | custom fusion | bytes 4198400 | tf_op jit(solution)/shard_map/jit(_take)/gather | solution.py:80
  131.3 2.6 copy.23
  133.8 1.8 broadcast_select_fusion.2
  135.6 0.0 copy-start.3
  135.6 2.6 copy.24
  138.3 0.0 copy-done.3
  138.3 6.8 %abs_reduce_fusion = (f32[1024]{0:T(1024)S(1)}, f32[1024,1024]{0,1:T(8,128)}) fusion(bf16[1024,1024]{1,0:T(8,128)(2,1)} %copy.24, bf16[1024,1024]{0,1:T(8,128)(2,1)S(1)} %broadcast_select_fusion.2, pred[]{:T(512)S(6)} %eq.16, f32[1024,1024]{0,1:T(8,128)} %copy.22), kind=kOutput, calls=%fused_computation.15 | convolution fusion | flops 2153774080 | bytes 12587009 | tf_op jit(solution)/shard_map/dot_general | solution.py:82
  145.1 0.6 reduce_max.9
  145.7 6.5 %fusion.3 = bf16[1024,1024]{1,0:T(8,128)(2,1)S(1)} fusion(f32[1024,1024]{0,1:T(8,128)} %get-tuple-element.140, f32[]{:T(128)} %reduce_max.9), kind=kOutput, calls=%fused_computation.19 | convolution fusion | flops 2153775104 | bytes 6291460 | tf_op jit(solution)/shard_map/dot_general | solution.py:43
  152.2 3.7 %fusion.63 = bf16[1024,1024]{1,0:T(8,128)(2,1)} fusion(bf16[1024,1024]{1,0:T(8,128)(2,1)S(1)} %fusion.3), kind=kOutput, calls=%fused_computation.162 | convolution fusion | flops 2147483648 | bytes 4194304 | tf_op jit(solution)/shard_map/dot_general | solution.py:46
  156.5 9.2 %fusion.25 = bf16[1024,1024]{1,0:T(8,128)(2,1)S(1)} fusion(f32[]{:T(128)S(6)} %mul.97, bf16[1024,1024]{1,0:T(8,128)(2,1)} %fusion.63, f32[1024,1024]{0,1:T(8,128)} %get-tuple-element.140, f32[]{:T(128)} %reduce_max.9), kind=kOutput, calls=%fused_computation.47 | convolution fusion | flops 4309647360 | bytes 8388616 | tf_op jit(solution)/shard_map/dot_general | solution.py:39
  165.7 0.0 copy-start.5
  165.7 1.5 collective-permute-start.1
  167.2 0.1 add_clamp_fusion
  167.3 0.1 min.18
  167.4 0.1 min.16
  167.4 0.1 broadcast_compare_fusion
  167.5 0.1 lt.119
  167.7 0.0 copy-done.5
  167.7 3.4 %collective-permute-done.1 = bf16[1024,1024]{1,0:T(8,128)(2,1)} collective-permute-done((bf16[1024,1024]{1,0:T(8,128)(2,1)S(1)}, bf16[1024,1024]{1,0:T(8,128)(2,1)}, u32[]{:S(2)}, u32[]{:S(2)}) %collective-permute-start.1) | collective-permute-done | bytes 2097184 | tf_op jit(solution)/shard_map/ppermute | solution.py:19
  171.1 1.8 broadcast_select_fusion.3
  172.9 5.6 %gather_fusion.3 = bf16[1024,1024]{1,0:T(8,128)(2,1)} fusion(bf16[1024,1024]{1,0:T(8,128)(2,1)S(1)} %broadcast_select_fusion.3, s32[1024]{0:T(1024)S(1)} %broadcast_clamp_fusion), kind=kCustom, calls=%fused_computation.3 | custom fusion | bytes 4198400 | tf_op jit(solution)/shard_map/jit(_take)/gather | solution.py:93
  178.5 4.1 %copy.26 = bf16[1024,1024]{0,1:T(8,128)(2,1)} copy(bf16[1024,1024]{1,0:T(8,128)(2,1)} %gather_fusion.3) | data formatting | bytes 4194304 | tf_op jit(solution)/shard_map/jit(_take)/gather | solution.py:93
  182.6 0.0 copy-done.4
  182.6 9.7 %multiply_reduce_fusion = (f32[]{:T(128)}, f32[1024,1024]{0,1:T(8,128)}) fusion(pred[1024]{0:T(1024)(128)(4,1)S(1)} %lt.119, bf16[1024,1024]{1,0:T(8,128)(2,1)} %collective-permute-done.1, bf16[1024,1024]{1,0:T(8,128)(2,1)} %copy-done.5, pred[]{:T(512)S(6)} %eq.16, bf16[1024,1024]{0,1:T(8,128)(2,1)S(1)} %copy-done.4, bf16[1024,1024]{0,1:T(8,128)(2,1)} %copy.26, ...), kind=kOutput, calls=%fused_computation.12 | convolution fusion | flops 4301258752 | bytes 12584965 | tf_op jit(solution)/shard_map/dot_general | solution.py:95
  192.3 9.1 %psum.28 = f32[]{:T(128)} all-reduce(f32[]{:T(128)} %get-tuple-element.141), channel_id=1, replica_groups=mesh['dp_0'=4,'dp_1'=8,'dp_2'=2,'mp'=4] {'dp_0'}, use_global_device_ids=true, to_apply=%region_6.7 | all-reduce | flops 1 | bytes 8 | tf_op jit(solution)/shard_map/psum | solution.py:23
  201.4 11.6 %psum.29 = f32[]{:T(128)} all-reduce(f32[]{:T(128)} %psum.28), channel_id=1, replica_groups=mesh['dp_0'=4,'dp_1'=8,'dp_2'=2,'mp'=4] {'dp_1'}, use_global_device_ids=true, to_apply=%region_7.8 | all-reduce | flops 1 | bytes 8 | tf_op jit(solution)/shard_map/psum | solution.py:23
  212.9 8.9 %psum.30 = f32[]{:T(128)} all-reduce(f32[]{:T(128)} %psum.29), channel_id=1, replica_groups=mesh['dp_0'=4,'dp_1'=8,'dp_2'=2,'mp'=4] {'dp_2'}, use_global_device_ids=true, to_apply=%region_8.9 | all-reduce | flops 1 | bytes 8 | tf_op jit(solution)/shard_map/psum | solution.py:23
  221.8 9.3 %psum.31 = f32[]{:T(128)} all-reduce(f32[]{:T(128)} %psum.30), channel_id=1, replica_groups=mesh['dp_0'=4,'dp_1'=8,'dp_2'=2,'mp'=4] {'mp'}, use_global_device_ids=true, to_apply=%region_9.10 | all-reduce | flops 1 | bytes 8 | tf_op jit(solution)/shard_map/psum | solution.py:23
  231.8 2.8 multiply_convert_fusion
  234.6 2.6 copy.28
  237.2 7.0 %all-to-all-start.1 = ((bf16[64,16,1024]{2,1,0:T(8,128)(2,1)}), bf16[64,16,1024]{2,1,0:T(8,128)(2,1)S(1)}, u32[]{:S(2)}, u32[]{:S(2)}) async-start(bf16[64,16,1024]{2,1,0:T(8,128)(2,1)} %bitcast.91), calls=%async_computation.1 | async-start | bytes 4194304 | tf_op jit(solution)/shard_map/all_to_all | solution.py:102
  244.2 0.0 copy-done.7
  244.2 5.3 %copy.29 = f32[1024,1024]{1,0:T(8,128)} copy(f32[1024,1024]{0,1:T(8,128)} %get-tuple-element.140) | data formatting | bytes 8388608
  249.6 45.8 %all-to-all-done.1 = bf16[64,16,1024]{2,1,0:T(8,128)(2,1)S(1)} async-done(((bf16[64,16,1024]{2,1,0:T(8,128)(2,1)}), bf16[64,16,1024]{2,1,0:T(8,128)(2,1)S(1)}, u32[]{:S(2)}, u32[]{:S(2)}) %all-to-all-start.1) | async-done | bytes 2097184 | tf_op jit(solution)/shard_map/all_to_all | solution.py:102
  295.4 1.3 copy-done.2
  296.7 0.6 gather_fusion.4
  297.3 0.0 copy-start.1
  297.3 3.3 %gather_fusion.5 = bf16[32,16,1024]{2,1,0:T(8,128)(2,1)} fusion(bf16[64,16,1024]{2,1,0:T(8,128)(2,1)} %copy-done.2, s32[1024]{0:T(1024)S(1)} %get-tuple-element.143), kind=kCustom, calls=%fused_computation.5 | custom fusion | bytes 2097280 | tf_op jit(solution)/shard_map/gather | solution.py:103
  300.7 2.8 pad_maximum_fusion.1
  303.5 0.0 copy-done.1
  (17 shorter events, 0.1 us)
Async XLA Ops:
  0.6 1.8 copy-start
  4.4 64.7 %copy-start.6 = (s32[64]{0:T(128)S(1)}, s32[64]{0:T(128)}, u32[]{:S(2)}) copy-start(s32[64]{0:T(128)} %param.6) | copy-start | bytes 772
  68.7 50.1 %collective-permute-start = (bf16[64,16,1024]{2,1,0:T(8,128)(2,1)S(1)}, bf16[64,16,1024]{2,1,0:T(8,128)(2,1)}, u32[]{:S(2)}, u32[]{:S(2)}) collective-permute-start(bf16[64,16,1024]{2,1,0:T(8,128)(2,1)S(1)} %all_to_all.10), channel_id=1, source_target_pairs={{0,4},{4,0},{8,12},{12,8},{16,20},{20,16},{24,28},{28,24},{32,36},... | collective-permute-start | bytes 6291464 | tf_op jit(solution)/shard_map/ppermute | solution.py:19
  135.6 2.6 copy-start.3
  165.7 1.9 copy-start.5
  165.7 5.4 %collective-permute-start.1 = (bf16[1024,1024]{1,0:T(8,128)(2,1)S(1)}, bf16[1024,1024]{1,0:T(8,128)(2,1)}, u32[]{:S(2)}, u32[]{:S(2)}) collective-permute-start(bf16[1024,1024]{1,0:T(8,128)(2,1)S(1)} %fusion.25), channel_id=1, source_target_pairs={{0,4},{4,0},{8,12},{12,8},{16,20},{20,16},{24,28},{28,24},{32,36},... | collective-permute-start | bytes 6291464 | tf_op jit(solution)/shard_map/ppermute | solution.py:19
  178.5 4.1 %copy-start.4 = (bf16[1024,1024]{0,1:T(8,128)(2,1)S(1)}, bf16[1024,1024]{0,1:T(8,128)(2,1)}, u32[]{:S(2)}) copy-start(bf16[1024,1024]{0,1:T(8,128)(2,1)} %copy-done.3) | copy-start | bytes 6291460
  237.2 7.0 %copy-start.7 = (s32[32]{0:T(128)S(1)}, s32[32]{0:T(128)}, u32[]{:S(2)}) copy-start(s32[32]{0:T(128)} %param.7) | copy-start | bytes 388
  237.2 58.2 %all-to-all-start.1 = ((bf16[64,16,1024]{2,1,0:T(8,128)(2,1)}), bf16[64,16,1024]{2,1,0:T(8,128)(2,1)S(1)}, u32[]{:S(2)}, u32[]{:S(2)}) async-start(bf16[64,16,1024]{2,1,0:T(8,128)(2,1)} %bitcast.91), calls=%async_computation.1 | async-start | bytes 4194304 | tf_op jit(solution)/shard_map/all_to_all | solution.py:102
  295.4 1.3 copy-start.2
  297.3 6.2 %copy-start.1 = (bf16[32,32,1024]{2,1,0:T(8,128)(2,1)S(1)}, bf16[32,32,1024]{2,1,0:T(8,128)(2,1)}, u32[]{:S(2)}) copy-start(bf16[32,32,1024]{2,1,0:T(8,128)(2,1)} %param.4) | copy-start | bytes 6291460
where the time goes:
time: 305 us; the launch traced here: 303 us
  blocking collectives  103 us (34%)
  other arithmetic  57 us (19%)
  waiting for transfers between devices  49.3 us (16%)
  local copies, waits for them, and re-layouts  47.2 us (15%)
  matrix products  35.8 us (12%)
  starting transfers between devices  8.84 us (3%)
    all_to_all x1, blocking collectives, body(): lax.all_to_all(outgoing, DP, split_axis=0, concat_axis=0, tiled=True)  64.3 us
    all_to_all x1, waiting for transfers between devices, body(): lax.all_to_all(outgoing_back, DP, split_axis=0, concat_axis=0, tiled=True)  45.8 us
    psum x4, blocking collectives, by_axis(): return functools.reduce(lax.psum, axes, array)  38.8 us
    and x1, other arithmetic, body(): jnp.take(received.reshape(devices * slot_rows, block_size), gather_rows,...  36 us
    unnamed x18, local copies, waits for them, and re-layouts  12.1 us
    gather x2, local copies, waits for them, and re-layouts, body(): jnp.take(received.reshape(devices * slot_rows, block_size), gather_rows,...  10.3 us
    gather x2, local copies, waits for them, and re-layouts, body(): jnp.take(left_root, jnp.clip(targets, 0, block_size - 1).reshape(-1), axi...  9.71 us
    dot_general x1, matrix products, body(): jnp.dot(half_prod, right_root, preferred_element_type=jnp.float32)  9.66 us
  transfers between devices with their start and end apart: 3, of which 2 were waited for; matrix products, arithmetic and copies ran while one was open for 18% of the time, Pallas kernels for 0%

commit v1 on v0

v1 whole, which is shorter than its diff:
```python
import functools

import jax
import jax.numpy as jnp
from jax import lax
from jax.experimental import pallas as pl
from jax.experimental.pallas import tpu as pltpu
from jax.sharding import Mesh
from jax.sharding import PartitionSpec as P

DP = ("dp_0", "dp_1", "dp_2")
BLK = 1024
TILE = 256
F32 = jnp.float32
BF16 = jnp.bfloat16

decay_rate = 0.95
epsilon = 1e-06


def place():
    return (
        lax.axis_index("dp_0"),
        lax.axis_index("dp_1"),
        lax.axis_index("dp_2"),
        lax.axis_index("mp"),
    )


def distance(step):
    odd = step % 2
    return (4 + odd * ((step + 1) // 2) - (1 - odd) * (step // 2)) % 8


def dot(a, b, dims=((1,), (0,))):
    return lax.dot_general(a, b, (dims, ((), ())), preferred_element_type=F32)


def greet(peers):
    barrier = pltpu.get_barrier_semaphore()
    for peer in peers:
        pl.semaphore_signal(barrier, inc=1, device_id=peer)
    return barrier, len(peers)


def block_peers(x, z, c):
    peers = []
    for dx in range(4):
        for dz in range(8):
            for dc in range(2):
                if dx or dz or dc:
                    peers.append(
                        {"dp_0": (x + dx) % 4, "dp_1": (z + dz) % 8, "dp_2": (c + dc) % 2}
                    )
    return peers


def drain(ref, send_sem, recv_sem, c):
    return pltpu.make_async_remote_copy(
        ref, ref, send_sem, recv_sem, device_id={"dp_2": (c + 1) % 2}
    )


def forward_kernel(
    o_ref, t_ref, g_ref, recv, acc, send_sem, recv_sem, psend_sem, precv_sem, loc_sem
):
    x, z, c, _ = place()
    barrier, count = greet(block_peers(x, z, c))
    acc[...] = jnp.zeros_like(acc)
    pl.semaphore_wait(barrier, count)
    mine = 16 * (2 * x + c)

    def send_one(step, dist, dx, dc):
        tx, tz, tc = (x + dx) % 4, (z + dist) % 8, (c + dc) % 2
        pltpu.make_async_remote_copy(
            o_ref.at[tx * 8 + tz, pl.ds(pl.multiple_of(16 * tc, 16), 16), :],
            recv.at[step, pl.ds(pl.multiple_of(mine, 16), 16), :],
            send_sem.at[step],
            recv_sem.at[step],
            device_id={"dp_0": tx, "dp_1": tz, "dp_2": tc},
        ).start()

    @pl.loop(0, 7)
    def _(step):
        for dx in range(4):
            for dc in range(2):
                send_one(step, distance(step), dx, dc)

    for dx in range(4):
        for dc in range(2):
            if dx or dc:
                send_one(7, 0, dx, dc)
    own = pltpu.make_async_copy(
        o_ref.at[x * 8 + z, pl.ds(pl.multiple_of(16 * c, 16), 16), :],
        recv.at[7, pl.ds(pl.multiple_of(mine, 16), 16), :],
        loc_sem,
    )
    own.start()

    def to_partner(step):
        return pltpu.make_async_remote_copy(
            recv.at[step, pl.ds(0, 128), :],
            recv.at[step, pl.ds(128, 128), :],
            psend_sem.at[step],
            precv_sem.at[step],
            device_id={"dp_2": (c + 1) % 2},
        )

    rows = lax.broadcasted_iota(jnp.int32, (TILE, 128), 0)

    def put(step):
        to_partner(step).wait_recv()
        zs = (z + 8 - distance(step)) % 8
        near = t_ref[pl.ds(zs * 2 + c, 1), :]
        far = t_ref[pl.ds(zs * 2 + (c + 1) % 2, 1), :]
        chunk = recv[step]

        @pl.loop(0, BLK // TILE)
        def _(tile):
            at = rows + tile * TILE
            pick = jnp.concatenate([at == near, at == far], axis=1)
            pick = jnp.where(pick, 1.0, 0.0).astype(BF16)
            here = pl.ds(pl.multiple_of(tile * TILE, TILE), TILE)
            acc[here, :] += dot(pick, chunk)

    def take(step, rows_in):
        drain(recv.at[step, pl.ds(0, rows_in), :], send_sem.at[step], recv_sem.at[step], c).wait_recv()

    take(0, 128)
    to_partner(0).start()

    @pl.loop(1, 7)
    def _(step):
        take(step, 128)
        to_partner(step).start()
        put(step - 1)

    take(7, 112)
    own.wait()
    to_partner(7).start()
    put(6)
    put(7)

    @pl.loop(0, BLK // TILE)
    def _(tile):
        here = pl.ds(pl.multiple_of(tile * TILE, TILE), TILE)
        g_ref[here, :] = acc[here, :].astype(BF16)

    @pl.loop(0, 8)
    def _(step):
        to_partner(step).wait_send()

    @pl.loop(0, 7)
    def _(step):
        drain(recv.at[step, pl.ds(0, 128), :], send_sem.at[step], recv_sem.at[step], c).wait_send()

    drain(recv.at[7, pl.ds(0, 112), :], send_sem.at[7], recv_sem.at[7], c).wait_send()


def root_kernel(
    g_ref, s_ref, a_out, root_ref, a, poly, root, moment, work, fourth, in_sem, out_sem
):
    c = lax.axis_index("dp_2")
    tiles = BLK // TILE

    def span(tile):
        return pl.ds(pl.multiple_of(tile * TILE, TILE), TILE)

    def fetch(tile):
        return pltpu.make_async_copy(s_ref.at[span(tile), :], a.at[span(tile), :], in_sem.at[tile])

    def flush(tile):
        return pltpu.make_async_copy(a.at[span(tile), :], a_out.at[span(tile), :], out_sem.at[tile])

    for tile in range(tiles):
        fetch(tile).start()

    def gram(side):
        def step(tile, total):
            if side == 0:
                prod = dot(g_ref[span(tile), :], g_ref[...], ((1,), (1,)))
            else:
                prod = dot(g_ref[:, span(tile)], g_ref[...], ((0,), (0,)))
            fetch(tile).wait()
            new = decay_rate * a[span(tile), :] + (1.0 - decay_rate) * prod
            a[span(tile), :] = new
            return total + jnp.sum(jnp.abs(new).reshape(TILE // 8, 8, BLK), axis=0)

        total = lax.fori_loop(0, tiles, step, jnp.zeros((8, BLK), F32))
        work[pl.ds(0, 8), :] = total

    pl.when(c == 0)(lambda: gram(0))
    pl.when(c == 1)(lambda: gram(1))
    for tile in range(tiles):
        flush(tile).start()
    bound = jnp.max(jnp.sum(work[pl.ds(0, 8), :], axis=0, keepdims=True), axis=1, keepdims=True)
    scale = 1.0 / bound
    factor = lax.rsqrt(jnp.sqrt(bound))
    row = lax.broadcasted_iota(jnp.int32, (TILE, BLK), 0)
    col = lax.broadcasted_iota(jnp.int32, (TILE, BLK), 1)

    def eye5(tile):
        return jnp.where(row + tile * TILE == col, 5.0, 0.0)

    @pl.loop(0, tiles)
    def _(tile):
        first = a[span(tile), :] * scale
        shifted = (eye5(tile) - first) * 0.25
        moment[span(tile), :] = first.astype(BF16)
        poly[span(tile), :] = shifted.astype(BF16)
        root[span(tile), :] = (factor * shifted).astype(BF16)

    work16 = fourth.at[0]
    four = fourth.at[1]

    @pl.loop(0, tiles)
    def _(tile):
        work16[span(tile), :] = dot(poly[span(tile), :], poly[...]).astype(BF16)

    @pl.loop(0, tiles)
    def _(tile):
        four[span(tile), :] = dot(work16[span(tile), :], work16[...]).astype(BF16)

    @pl.loop(0, tiles)
    def _(tile):
        new = dot(four[span(tile), :], moment[...])
        poly[span(tile), :] = ((eye5(tile) - new) * 0.25).astype(BF16)

    @pl.loop(0, tiles)
    def _(tile):
        root_ref[span(tile), :] = dot(root[span(tile), :], poly[...]).astype(BF16)

    for tile in range(tiles):
        flush(tile).wait()


def backward_kernel(
    entries,
    root_ref,
    g_ref,
    t_ref,
    f_ref,
    scale_ref,
    roots,
    ways,
    square,
    small,
    ring,
    loc_sem,
    root_sem,
    send_sem,
    recv_sem,
    near_sem,
    sum_send,
    sum_recv,
):
    x, z, c, y = place()
    partner = {"dp_2": (c + 1) % 2}
    peers = block_peers(x, z, c) + [{"mp": (y + dy) % 4} for dy in range(1, 4)]
    barrier, count = greet(peers)
    keep = pltpu.make_async_copy(root_ref, roots.at[c], loc_sem.at[0])
    keep.start()
    square[...] = jnp.zeros_like(square)
    pl.semaphore_wait(barrier, count)
    swap = pltpu.make_async_remote_copy(
        root_ref, roots.at[c], root_sem.at[0], root_sem.at[1], device_id=partner
    )
    swap.start()
    keep.wait()
    swap.wait_recv()
    cols = lax.broadcasted_iota(jnp.int32, (128, BLK), 1).astype(F32)

    def wanted(step):
        zt = (z + distance(step)) % 8
        line = t_ref[pl.ds(zt * 2 + c, 1), :].astype(F32)
        turned = jnp.transpose(jnp.broadcast_to(line, (128, 128)))
        return jnp.where(jnp.concatenate([turned] * 8, axis=1) == cols, 1.0, 0.0).astype(BF16)

    def make(pair):
        pick = jnp.concatenate([wanted(2 * pair), wanted(2 * pair + 1)], axis=0)
        picked = dot(pick, roots[0]).astype(BF16)
        half = dot(picked, g_ref[...]).astype(BF16)
        full = dot(half, roots[1])
        ways[pl.ds(pl.multiple_of(pair * 256, 256), 256), :] = full.astype(BF16)
        square[...] += jnp.sum((full * full).reshape(32, 8, BLK), axis=0)

    slot = pl.ds(pl.multiple_of(16 * c, 16), 16)

    def send_one(step, dist, dx, dc, ssem, rsem):
        tx, tz, tc = (x + dx) % 4, (z + dist) % 8, (c + dc) % 2
        return pltpu.make_async_remote_copy(
            ways.at[pl.ds(pl.multiple_of(step * 128 + 16 * (2 * tx + tc), 16), 16), :],
            f_ref.at[x * 8 + z, slot, :],
            ssem,
            rsem,
            device_id={"dp_0": tx, "dp_1": tz, "dp_2": tc},
        )

    def send_step(step):
        for dx in range(4):
            for dc in range(2):
                send_one(step, distance(step), dx, dc, send_sem, recv_sem).start()

    @pl.loop(0, 2)
    def _(pair):
        make(pair)
        send_step(2 * pair)
        send_step(2 * pair + 1)

    @pl.loop(2, 4)
    def _(pair):
        make(pair)

    own = jnp.sum(square[...], axis=0, keepdims=True)
    part = own[:, 0:128]
    for i in range(1, 8):
        part = part + own[:, 128 * i : 128 * (i + 1)]
    one = pl.ds(0, 1)
    small[0, one, :] = part
    pair_sum = pltpu.make_async_remote_copy(
        small.at[0, one, :], small.at[3, one, :], sum_send.at[0], sum_recv.at[0], device_id=partner
    )
    pair_sum.start()
    pair_sum.wait_recv()
    part = part + small[3, one, :]
    small[1, one, :] = part
    for dy in range(1, 4):
        pltpu.make_async_remote_copy(
            small.at[1, one, :],
            small.at[3 + dy, one, :],
            sum_send.at[1],
            sum_recv.at[1],
            device_id={"mp": (y + dy) % 4},
        ).start()
    three = pltpu.make_async_remote_copy(
        small.at[pl.ds(4, 3), one, :],
        small.at[pl.ds(4, 3), one, :],
        sum_send.at[1],
        sum_recv.at[1],
        device_id={"mp": (y + 1) % 4},
    )
    three.wait_recv()
    for dy in range(1, 4):
        part = part + small[3 + dy, one, :]
    small[2, one, :] = part
    for dx in range(4):
        for dz in range(8):
            if dx or dz:
                pltpu.make_async_remote_copy(
                    small.at[2, one, :],
                    ring.at[dx * 8 + dz - 1, one, :],
                    sum_send.at[2],
                    sum_recv.at[2],
                    device_id={"dp_0": (x + dx) % 4, "dp_1": (z + dz) % 8},
                ).start()

    send_step(4)
    send_step(5)
    send_step(6)
    last = []
    for dx in range(4):
        for dc in range(2):
            if dx == 0 and dc == 0:
                continue
            if dx == 0:
                last.append(send_one(7, 0, dx, dc, near_sem.at[0], near_sem.at[1]))
            else:
                last.append(send_one(7, 0, dx, dc, send_sem, recv_sem))
            last[-1].start()
    stay = pltpu.make_async_copy(
        ways.at[pl.ds(pl.multiple_of(7 * 128 + 16 * (2 * x + c), 16), 16), :],
        f_ref.at[x * 8 + z, slot, :],
        loc_sem.at[1],
    )
    stay.start()
    everyone = pltpu.make_async_remote_copy(
        ring.at[pl.ds(0, 31), one, :],
        ring.at[pl.ds(0, 31), one, :],
        sum_send.at[2],
        sum_recv.at[2],
        device_id=partner,
    )
    everyone.wait_recv()
    for i in range(31):
        part = part + ring[i, one, :]
    mean = jnp.sum(part, axis=1, keepdims=True) * (1.0 / entries)
    scale_ref[...] = jnp.broadcast_to(lax.rsqrt(mean + epsilon), (8, 128))

    swap.wait_send()
    pair_sum.wait_send()
    three.wait_send()
    everyone.wait_send()
    stay.wait()
    last[0].wait_send()
    last[0].wait_recv()
    bulk = pltpu.make_async_remote_copy(
        ways.at[pl.ds(0, 992), :], ways.at[pl.ds(0, 992), :], send_sem, recv_sem, device_id=partner
    )
    bulk.wait_send()
    bulk.wait_recv()


VMEM = pl.BlockSpec(memory_space=pltpu.VMEM)
ANY = pl.BlockSpec(memory_space=pl.ANY)
DMA = pltpu.SemaphoreType.DMA


def shape(dims, kind):
    return jax.ShapeDtypeStruct(dims, kind)


def body(gradients, statistics, row_counts, block_pair):
    blocks, slots, _ = gradients.shape
    devices = lax.axis_size(DP)
    ids = jnp.arange(devices // 2, dtype=jnp.int32)
    block_of = jnp.sum(jnp.where(block_pair[None, :] == ids[:, None], ids[None, :], 0), axis=1)
    outgoing = jnp.take(gradients, block_of, axis=0, mode="clip")
    peers = jnp.arange(devices, dtype=jnp.int32)
    before = peers[None, :] < peers[:, None]
    offsets = jnp.sum(jnp.where(before, row_counts[None, :], 0), axis=1)
    slot_ids = jnp.arange(slots, dtype=jnp.int32)
    table = jnp.where(
        slot_ids[None, :] < row_counts[:, None], offsets[:, None] + slot_ids[None, :], -1
    )
    table = table.reshape(4, 8, 2, 2, 16).transpose(1, 3, 0, 2, 4).reshape(16, 128)

    grad = pl.pallas_call(
        forward_kernel,
        out_shape=shape((BLK, BLK), BF16),
        in_specs=[ANY, VMEM],
        out_specs=VMEM,
        scratch_shapes=[
            pltpu.VMEM((8, 256, BLK), BF16),
            pltpu.VMEM((BLK, BLK), F32),
            DMA((8,)),
            DMA((8,)),
            DMA((8,)),
            DMA((8,)),
            DMA,
        ],
        compiler_params=pltpu.CompilerParams(
            collective_id=0, has_side_effects=True, vmem_limit_bytes=48 << 20
        ),
        name="forward",
    )(outgoing, table)

    accumulated, root = pl.pallas_call(
        root_kernel,
        out_shape=(shape((BLK, BLK), F32), shape((BLK, BLK), BF16)),
        in_specs=[VMEM, ANY],
        out_specs=(ANY, VMEM),
        scratch_shapes=[
            pltpu.VMEM((BLK, BLK), F32),
            pltpu.VMEM((BLK, BLK), BF16),
            pltpu.VMEM((BLK, BLK), BF16),
            pltpu.VMEM((BLK, BLK), BF16),
            pltpu.VMEM((8, BLK), F32),
            pltpu.VMEM((2, BLK, BLK), BF16),
            DMA((4,)),
            DMA((4,)),
        ],
        compiler_params=pltpu.CompilerParams(vmem_limit_bytes=48 << 20),
        name="roots",
    )(grad, statistics)

    entries = lax.axis_size("mp") * blocks * BLK * BLK
    returned, scale = pl.pallas_call(
        functools.partial(backward_kernel, entries),
        out_shape=(shape((blocks, slots, BLK), BF16), shape((8, 128), F32)),
        in_specs=[ANY, VMEM, VMEM],
        out_specs=(ANY, VMEM),
        scratch_shapes=[
            pltpu.VMEM((2, BLK, BLK), BF16),
            pltpu.VMEM((BLK, BLK), BF16),
            pltpu.VMEM((8, BLK), F32),
            pltpu.VMEM((8, 8, 128), F32),
            pltpu.VMEM((32, 8, 128), F32),
            DMA((2,)),
            DMA((2,)),
            DMA,
            DMA,
            DMA((2,)),
            DMA((3,)),
            DMA((3,)),
        ],
        compiler_params=pltpu.CompilerParams(
            collective_id=1, has_side_effects=True, vmem_limit_bytes=48 << 20
        ),
        name="backward",
    )(root, grad, table)

    update = (jnp.take(returned, block_pair, axis=0, mode="clip").astype(F32) * scale[0, 0]).astype(BF16)
    return (update, accumulated)


def solution(mesh):
    torus = Mesh(mesh.devices.reshape(4, 8, 2, mesh.shape["mp"]), DP + ("mp",))
    placed = (P(None, DP, "mp"), P(DP, "mp"), P(), P())
    return jax.shard_map(
        body,
        mesh=torus,
        in_specs=placed,
        out_specs=(P(None, DP, "mp"), P(DP, "mp")),
        check_vma=False,
    )
```

time: 305 us -> 163 us (0.53)
  Pallas kernels: 0 us -> 146 us
  blocking collectives: 103 us -> 0 us
  other arithmetic: 57 us -> 5.95 us
  waiting for transfers between devices: 49.3 us -> 0 us
  local copies, waits for them, and re-layouts: 47.2 us -> 10.1 us
  matrix products: 35.8 us -> 0 us
  starting transfers between devices: 8.84 us -> 0 us
    pallas_call x0 -> x3, Pallas kernels: none -> 146 us  [the longest x1 65.6 us: body(): pl.pallas_call(forward_kernel, out_shape=shape((BLK, BLK), BF16), in_spec...]
    all_to_all x1 -> x0, blocking collectives: 64.3 us -> none  [body(): lax.all_to_all(outgoing, DP, split_axis=0, concat_axis=0, tiled=True)]
    all_to_all x1 -> x0, waiting for transfers between devices: 45.8 us -> none  [body(): lax.all_to_all(outgoing_back, DP, split_axis=0, concat_axis=0, tiled=True)]
    psum x4 -> x0, blocking collectives: 38.8 us -> none  [by_axis(): return functools.reduce(lax.psum, axes, array)]
    and x2 -> x0, other arithmetic: 36 us -> none  [the longest x1 36 us: body(): jnp.take(received.reshape(devices * slot_rows, block_size), gather_rows,...]
    dot_general x5 -> x0, matrix products: 35.8 us -> none  [the longest x1 9.66 us: body(): jnp.dot(half_prod, right_root, preferred_element_type=jnp.float32)]
    gather x12 -> x2, local copies, waits for them, and re-layouts: 29.6 us -> 5.61 us  [the longest x1 3.61 us: body(): jnp.take(returned, block_pair, axis=0, mode='clip').astype(F32)]
    unnamed x18 -> x10, local copies, waits for them, and re-layouts: 12.1 us -> 2.93 us
  transfers between devices with their start and end apart: 3 -> 0, of which waited for: 2 -> 0; matrix products, arithmetic and copies ran while one was open for 18% -> 0% of each run, Pallas kernels for 0% -> 0%
where the time goes in v1:
time: 163 us
  Pallas kernels  146 us (90%)
  local copies, waits for them, and re-layouts  10.1 us (6%)
  other arithmetic  5.95 us (4%)
    pallas_call x1, Pallas kernels, body(): pl.pallas_call(forward_kernel, out_shape=shape((BLK, BLK), BF16), in_spec...  65.6 us
    pallas_call x1, Pallas kernels, body(): pl.pallas_call(functools.partial(backward_kernel, entries), out_shape=(sh...  62.1 us
    pallas_call x1, Pallas kernels, body(): pl.pallas_call(root_kernel, out_shape=(shape((BLK, BLK), F32), shape((BLK...  18.1 us
    convert_element_type x1, other arithmetic, body(): (jnp.take(returned, block_pair, axis=0, mode='clip').astype(F32) * scale[...  4.11 us
    gather x1, local copies, waits for them, and re-layouts, body(): jnp.take(returned, block_pair, axis=0, mode='clip').astype(F32)  3.61 us

profile of v1, /device:TPU:1, one launch (start us, length us, event | category | flops | bytes accessed | tf_op | source)
XLA Modules:
  0.0 162.6 jit_solution(7819477617626671943)
XLA Ops:
  0.6 0.0 copy-start
  0.6 0.9 select_reduce_fusion
  1.6 0.1 add.24
  1.7 0.8 lt.50
  2.5 0.1 compare_select_fusion
  2.6 0.1 select_n.21.t_ref
  2.7 0.8 select_reduce_fusion.1
  3.5 0.0 copy-done
  3.5 2.0 %gather_fusion = bf16[32,32,1024]{2,1,0:T(8,128)(2,1)} fusion(bf16[32,32,1024]{2,1,0:T(8,128)(2,1)S(1)} %copy-done, s32[1024]{0:T(1024)S(1)} %pad_clamp_fusion.1), kind=kCustom, calls=%fused_computation | custom fusion | bytes 4194432 | tf_op jit(solution)/shard_map/jit(_take)/gather | solution.py:417
  5.5 0.0 copy-start.2
  5.5 1.6 copy-done.2
  7.1 65.6 %forward.1.g_ref = bf16[1024,1024]{1,0:T(8,128)(2,1)S(1)} custom-call(bf16[32,32,1024]{2,1,0:T(8,128)(2,1)S(1)} %copy-done.2, s32[16,128]{1,0:T(8,128)S(1)} %select_n.21.t_ref), custom_call_target="tpu_custom_call" | custom-call | tf_op jit(solution)/shard_map/forward/pallas_call | solution.py:427
  72.7 0.0 copy-start.1
  72.7 18.1 %roots.1 = (f32[1024,1024]{1,0:T(8,128)}, bf16[1024,1024]{1,0:T(8,128)(2,1)S(1)}) custom-call(bf16[1024,1024]{1,0:T(8,128)(2,1)S(1)} %forward.1.g_ref, f32[1024,1024]{1,0:T(8,128)} %s_ref.1), custom_call_target="tpu_custom_call" | custom-call | tf_op jit(solution)/shard_map/roots/pallas_call | solution.py:447
  90.8 0.0 copy-done.1
  90.8 0.0 copy-start.4
  90.9 62.1 %backward.1 = (bf16[32,32,1024]{2,1,0:T(8,128)(2,1)S(1)}, f32[8,128]{1,0:T(8,128)S(1)}) custom-call(bf16[1024,1024]{1,0:T(8,128)(2,1)S(1)} %get-tuple-element.6.root_ref, bf16[1024,1024]{1,0:T(8,128)(2,1)} %copy-done.1, s32[16,128]{1,0:T(8,128)S(1)} %select_n.21.t_ref), custom_call_target="tpu_custom_call" | custom-call | tf_op jit(solution)/shard_map/backward/pallas_call | solution.py:467
  153.0 0.0 copy-start.3
  153.0 1.3 copy-done.3
  154.3 0.0 copy-done.4
  154.3 3.6 %gather_fusion.1 = bf16[32,32,1024]{2,1,0:T(8,128)(2,1)} fusion(bf16[32,32,1024]{2,1,0:T(8,128)(2,1)} %copy-done.3, s32[1024]{0:T(1024)S(1)} %pad_clamp_fusion), kind=kCustom, calls=%fused_computation.1 | custom fusion | bytes 4194432 | tf_op jit(solution)/shard_map/jit(_take)/gather | solution.py:492
  157.9 0.5 slice.3
  158.4 4.1 %multiply_convert_fusion = bf16[32,32,1024]{2,1,0:T(8,128)(2,1)} fusion(bf16[32,32,1024]{2,1,0:T(8,128)(2,1)} %gather_fusion.1, f32[]{:T(128)} %bitcast.2), kind=kLoop, calls=%fused_computation.2 | loop fusion | flops 3145728 | bytes 4194308 | tf_op jit(solution)/shard_map/convert_element_type | solution.py:492
  (5 shorter events, 0.0 us)
Async XLA Ops:
  0.6 2.9 %copy-start = (bf16[32,32,1024]{2,1,0:T(8,128)(2,1)S(1)}, bf16[32,32,1024]{2,1,0:T(8,128)(2,1)}, u32[]{:S(2)}) copy-start(bf16[32,32,1024]{2,1,0:T(8,128)(2,1)} %param.4) | copy-start | bytes 6291460
  5.5 1.6 copy-start.2
  72.7 18.1 %copy-start.1 = (bf16[1024,1024]{1,0:T(8,128)(2,1)}, bf16[1024,1024]{1,0:T(8,128)(2,1)S(1)}, u32[]{:S(2)}) copy-start(bf16[1024,1024]{1,0:T(8,128)(2,1)S(1)} %forward.1.g_ref) | copy-start | bytes 6291460
  90.8 63.5 %copy-start.4 = (s32[32]{0:T(128)S(1)}, s32[32]{0:T(128)}, u32[]{:S(2)}) copy-start(s32[32]{0:T(128)} %param.7) | copy-start | bytes 388
  153.0 1.3 copy-start.3

commit v2 on v0

v2 whole, which is shorter than its diff:
```python
import functools

import jax
import jax.numpy as jnp
from jax import lax
from jax.experimental import pallas as pl
from jax.experimental.pallas import tpu as pltpu
from jax.sharding import Mesh
from jax.sharding import PartitionSpec as P

DP = ("dp_0", "dp_1", "dp_2")
BLK = 1024
TILE = 256
F32 = jnp.float32
BF16 = jnp.bfloat16

decay_rate = 0.95
epsilon = 1e-06


def place():
    return (
        lax.axis_index("dp_0"),
        lax.axis_index("dp_1"),
        lax.axis_index("dp_2"),
        lax.axis_index("mp"),
    )


def distance(step):
    odd = step % 2
    return (4 + odd * ((step + 1) // 2) - (1 - odd) * (step // 2)) % 8


def dot(a, b, dims=((1,), (0,))):
    return lax.dot_general(a, b, (dims, ((), ())), preferred_element_type=F32)


def greet(peers):
    barrier = pltpu.get_barrier_semaphore()
    for peer in peers:
        pl.semaphore_signal(barrier, inc=1, device_id=peer)
    return barrier, len(peers)


def plane_peers(x, c):
    return [
        {"dp_0": (x + dx) % 4, "dp_2": (c + dc) % 2}
        for dx in range(4)
        for dc in range(2)
        if dx or dc
    ]


def z_peers(z):
    return [{"dp_1": (z + dz) % 8} for dz in range(1, 8)]


def transfer(ref, send_sem, recv_sem, c):
    return pltpu.make_async_remote_copy(
        ref, ref, send_sem, recv_sem, device_id={"dp_2": (c + 1) % 2}
    )


def half_of(c):
    return pl.ds(pl.multiple_of(512 * c, 512), 512)


def slots_of(x, c):
    return pl.ds(pl.multiple_of(32 * (2 * x + c), 32), 32)


def span(tile):
    return pl.ds(pl.multiple_of(tile * TILE, TILE), TILE)


def deal_kernel(counts, pair, g_ref, o_ref, t_ref):
    @pl.loop(0, 32)
    def _(k):
        o_ref[pair[k]] = g_ref[k]

    lane = lax.broadcasted_iota(jnp.int32, (8, 256), 1)
    plane = lax.broadcasted_iota(jnp.int32, (8, 256), 0)
    inner = lane % 32
    group = lane // 32
    spot = jnp.full((8, 256), -1, jnp.int32)
    target = jnp.full((8, 256), -1, jnp.int32)
    offset = counts[0] * 0
    filled = [offset] * 8
    for x in range(4):
        for z in range(8):
            for c in range(2):
                q = (x * 8 + z) * 2 + c
                n = counts[q]
                at = filled[z]
                here = (plane == z) & (group == 2 * x + c) & (inner < n)
                spot = jnp.where(here, at + inner, spot)
                held = (plane == z) & (lane >= at) & (lane < at + n)
                target = jnp.where(held, offset - at + lane, target)
                filled[z] = at + n
                offset = offset + n
    t_ref[0:8, :] = spot
    t_ref[8:16, :] = target


def forward_kernel(
    room,
    o_ref,
    t_ref,
    g_ref,
    near,
    packed,
    recv,
    acc,
    pick_ref,
    x_send,
    x_recv,
    z_send,
    z_recv,
    p_send,
    p_recv,
):
    x, z, c, _ = place()
    barrier, count = greet(plane_peers(x, c) + z_peers(z))
    spot = t_ref[pl.ds(z, 1), :]
    rows = lax.broadcasted_iota(jnp.int32, (256, 256), 0)
    pick_ref[...] = jnp.where(rows == spot, 1.0, 0.0).astype(BF16)
    pl.semaphore_wait(barrier, count)

    def give(step):
        tz = (z + distance(step)) % 8
        for dx in range(4):
            for dc in range(2):
                tx, tc = (x + dx) % 4, (c + dc) % 2
                if dx or dc:
                    pltpu.make_async_remote_copy(
                        o_ref.at[tx * 8 + tz, :, half_of(tc)],
                        near.at[step, slots_of(x, c), :],
                        x_send,
                        x_recv.at[step],
                        device_id={"dp_0": tx, "dp_2": tc},
                    ).start()

    @pl.loop(0, 8)
    def _(step):
        give(step)

    def keep(step):
        tz = (z + distance(step)) % 8
        near[step, slots_of(x, c), :] = o_ref[x * 8 + tz, :, half_of(c)]

    @pl.loop(0, 8)
    def _(step):
        keep(step)

    def pack(step):
        transfer(near.at[step, pl.ds(0, 224), :], x_send, x_recv.at[step], c).wait_recv()
        return dot(pick_ref[pl.ds(0, room), :], near[step]).astype(BF16)

    def to_partner(step):
        part = recv.at[step, :, half_of(c)]
        return pltpu.make_async_remote_copy(
            part, part, p_send.at[step], p_recv.at[step], device_id={"dp_2": (c + 1) % 2}
        )

    @pl.loop(0, 7)
    def _(step):
        packed[step] = pack(step)
        pltpu.make_async_remote_copy(
            packed.at[step],
            recv.at[step, :, half_of(c)],
            z_send,
            z_recv.at[step],
            device_id={"dp_1": (z + distance(step)) % 8},
        ).start()

    recv[7, :, half_of(c)] = pack(7)
    to_partner(7).start()
    lines = lax.broadcasted_iota(jnp.int32, (TILE, room), 0)

    def put(step, first=False, last=False):
        to_partner(step).wait_recv()
        zs = (z + 8 - distance(step)) % 8
        target = t_ref[pl.ds(8 + zs, 1), :][:, 0:room]

        @pl.loop(0, BLK // TILE)
        def _(tile):
            pick = jnp.where(lines + tile * TILE == target, 1.0, 0.0).astype(BF16)
            new = dot(pick, recv[step])
            if not first:
                new = acc[span(tile), :] + new
            if last:
                g_ref[span(tile), :] = new.astype(BF16)
            else:
                acc[span(tile), :] = new

    def take(step):
        transfer(packed.at[step], z_send, z_recv.at[step], c).wait_recv()
        to_partner(step).start()

    take(0)
    put(7, first=True)

    @pl.loop(1, 7)
    def _(step):
        take(step)
        put(step - 1)

    put(6, last=True)

    @pl.loop(0, 8)
    def _(step):
        to_partner(step).wait_send()

    transfer(near.at[pl.ds(0, 7)], x_send, x_recv.at[0], c).wait_send()
    transfer(packed, z_send, z_recv.at[0], c).wait_send()


def root_kernel(
    g_ref, s_ref, a_out, root, step_ref, a, poly, moment, work, fourth, in_sem, out_sem
):
    c = lax.axis_index("dp_2")
    tiles = BLK // TILE

    def fetch(tile):
        return pltpu.make_async_copy(s_ref.at[span(tile), :], a.at[span(tile), :], in_sem.at[tile])

    def flush(tile):
        return pltpu.make_async_copy(a.at[span(tile), :], a_out.at[span(tile), :], out_sem.at[tile])

    for tile in range(tiles):
        fetch(tile).start()

    def gram(side):
        def step(tile, total):
            if side == 0:
                prod = dot(g_ref[span(tile), :], g_ref[...], ((1,), (1,)))
            else:
                prod = dot(g_ref[:, span(tile)], g_ref[...], ((0,), (0,)))
            fetch(tile).wait()
            new = decay_rate * a[span(tile), :] + (1.0 - decay_rate) * prod
            a[span(tile), :] = new
            return total + jnp.sum(jnp.abs(new).reshape(TILE // 8, 8, BLK), axis=0)

        total = lax.fori_loop(0, tiles, step, jnp.zeros((8, BLK), F32))
        work[pl.ds(0, 8), :] = total

    pl.when(c == 0)(lambda: gram(0))
    pl.when(c == 1)(lambda: gram(1))
    for tile in range(tiles):
        flush(tile).start()
    bound = jnp.max(jnp.sum(work[pl.ds(0, 8), :], axis=0, keepdims=True), axis=1, keepdims=True)
    scale = 1.0 / bound
    factor = lax.rsqrt(jnp.sqrt(bound))
    row = lax.broadcasted_iota(jnp.int32, (TILE, BLK), 0)
    col = lax.broadcasted_iota(jnp.int32, (TILE, BLK), 1)

    def eye5(tile):
        return jnp.where(row + tile * TILE == col, 5.0, 0.0)

    @pl.loop(0, tiles)
    def _(tile):
        first = a[span(tile), :] * scale
        shifted = (eye5(tile) - first) * 0.25
        moment[span(tile), :] = first.astype(BF16)
        poly[span(tile), :] = shifted.astype(BF16)
        root[span(tile), :] = (factor * shifted).astype(BF16)

    work16 = fourth.at[0]
    four = fourth.at[1]

    @pl.loop(0, tiles)
    def _(tile):
        work16[span(tile), :] = dot(poly[span(tile), :], poly[...]).astype(BF16)

    @pl.loop(0, tiles)
    def _(tile):
        four[span(tile), :] = dot(work16[span(tile), :], work16[...]).astype(BF16)

    @pl.loop(0, tiles)
    def _(tile):
        new = dot(four[span(tile), :], moment[...])
        step_ref[span(tile), :] = ((eye5(tile) - new) * 0.25).astype(BF16)

    for tile in range(tiles):
        flush(tile).wait()


def backward_kernel(
    room,
    entries,
    root_ref,
    step_ref,
    g_ref,
    t_ref,
    f_ref,
    scale_ref,
    roots,
    ways,
    back,
    slots,
    spread_ref,
    square,
    told,
    heard,
    root_sem,
    z_send,
    z_recv,
    x_send,
    x_recv,
    sum_send,
    sum_recv,
):
    x, z, c, y = place()
    partner = {"dp_2": (c + 1) % 2}
    y_peers = [{"mp": (y + dy) % 4} for dy in range(1, 4)]
    x_peers = [{"dp_0": (x + dx) % 4} for dx in range(1, 4)]
    barrier, count = greet(plane_peers(x, c) + z_peers(z) + y_peers)

    def make_root(tile):
        roots[c, span(tile), :] = dot(root_ref[span(tile), :], step_ref[...]).astype(BF16)

    def swap(tile):
        part = roots.at[c, span(tile), :]
        return pltpu.make_async_remote_copy(
            part, part, root_sem.at[0], root_sem.at[1], device_id=partner
        )

    def column(line):
        turned = jnp.transpose(jnp.broadcast_to(line.astype(F32), (128, 256)))
        return jnp.concatenate([turned] * 8, axis=1)

    cols = lax.broadcasted_iota(jnp.int32, (256, BLK), 1).astype(F32)
    spread = jnp.where(column(t_ref[pl.ds(z, 1), :]) == cols, 1.0, 0.0)
    spread_ref[...] = spread[:, 0:256].astype(BF16)
    square[...] = jnp.zeros_like(square)

    @pl.loop(0, 2)
    def _(tile):
        make_root(tile)

    pl.semaphore_wait(barrier, count)
    swap(0).start()
    swap(1).start()

    @pl.loop(2, 4)
    def _(tile):
        make_root(tile)
        swap(tile).start()

    whole = transfer(roots.at[c], root_sem.at[0], root_sem.at[1], c)
    whole.wait_recv()

    def make(step):
        zt = (z + distance(step)) % 8
        want = column(t_ref[pl.ds(8 + zt, 1), :]) == cols
        pick = jnp.where(want, 1.0, 0.0).astype(BF16)[0:room, :]
        picked = dot(pick, roots[0]).astype(BF16)
        half = dot(picked, g_ref[...]).astype(BF16)
        full = dot(half, roots[1, :, half_of(c)])
        ways[step] = full.astype(BF16)
        square[...] += jnp.sum((full * full).reshape(room // 8, 8, 512), axis=0)

    @pl.loop(0, 7)
    def _(step):
        make(step)
        pltpu.make_async_remote_copy(
            ways.at[step],
            back.at[step],
            z_send,
            z_recv.at[step],
            device_id={"dp_1": (z + distance(step)) % 8},
        ).start()

    make(7)
    one = pl.ds(0, 1)

    def tell(stage, part, peers, at):
        told[stage, one, :] = part
        for i, peer in enumerate(peers):
            pltpu.make_async_remote_copy(
                told.at[stage, one, :],
                heard.at[at + i, one, :],
                sum_send.at[stage],
                sum_recv.at[stage],
                device_id=peer,
            ).start()

    def hear(stage, part, number, at):
        ref = heard.at[pl.ds(at, number), one, :]
        transfer(ref, sum_send.at[stage], sum_recv.at[stage], c).wait()
        for i in range(number):
            part = part + heard[at + i, one, :]
        return part

    def give(step, rows):
        slots[step] = dot(spread_ref[:, 0:room], rows).astype(BF16)
        block = x * 8 + (z + 8 - distance(step)) % 8
        for dx in range(4):
            for dc in range(2):
                tx, tc = (x + dx) % 4, (c + dc) % 2
                if dx or dc:
                    pltpu.make_async_remote_copy(
                        slots.at[step, slots_of(tx, tc), :],
                        f_ref.at[block, :, half_of(c)],
                        x_send,
                        x_recv,
                        device_id={"dp_0": tx, "dp_2": tc},
                    ).start()
        f_ref[block, :, half_of(c)] = slots[step, slots_of(x, c), :]

    def pass_on(step):
        transfer(back.at[step], z_send, z_recv.at[step], c).wait_recv()
        give(step, back[step])

    own = jnp.sum(square[...], axis=0, keepdims=True)
    part = own[:, 0:128] + own[:, 128:256] + own[:, 256:384] + own[:, 384:512]
    tell(0, part, [partner], 0)
    give(7, ways[7])
    part = hear(0, part, 1, 0)
    tell(1, part, y_peers, 1)
    pass_on(0)
    part = hear(1, part, 3, 1)
    tell(2, part, x_peers, 4)
    pass_on(1)
    part = hear(2, part, 3, 4)
    tell(3, part, z_peers(z), 7)

    @pl.loop(2, 7)
    def _(step):
        pass_on(step)

    part = hear(3, part, 7, 7)
    mean = jnp.sum(part, axis=1, keepdims=True) * (1.0 / entries)
    scale_ref[...] = jnp.broadcast_to(lax.rsqrt(mean + epsilon), (8, 128))
    whole.wait_send()
    transfer(ways.at[pl.ds(0, 7)], z_send, z_recv.at[0], c).wait_send()
    transfer(slots.at[pl.ds(0, 7)], x_send, x_recv, c).wait_send()
    transfer(f_ref.at[pl.ds(0, 28)], x_send, x_recv, c).wait_recv()


def finish_kernel(pair, scale_ref, f_ref, u_ref, held, sem):
    scale = scale_ref[0:1, 0:1]

    def flush(group):
        part = pl.ds(group * 8, 8)
        return pltpu.make_async_copy(held.at[part], u_ref.at[part], sem.at[group])

    @pl.loop(0, 4)
    def _(group):
        for i in range(8):
            k = group * 8 + i
            held[k] = (f_ref[pair[k]].astype(F32) * scale).astype(BF16)
        flush(group).start()

    for group in range(4):
        flush(group).wait()


VMEM = pl.BlockSpec(memory_space=pltpu.VMEM)
SMEM = pl.BlockSpec(memory_space=pltpu.SMEM)
ANY = pl.BlockSpec(memory_space=pl.ANY)
DMA = pltpu.SemaphoreType.DMA
LIMIT = 48 << 20
ROOM = 192
FULL = 256


def shape(dims, kind):
    return jax.ShapeDtypeStruct(dims, kind)


def remote(number):
    return pltpu.CompilerParams(
        collective_id=number, has_side_effects=True, vmem_limit_bytes=LIMIT
    )


def forward(room, number):
    return pl.pallas_call(
        functools.partial(forward_kernel, room),
        out_shape=shape((BLK, BLK), BF16),
        in_specs=[VMEM, VMEM],
        out_specs=VMEM,
        scratch_shapes=[
            pltpu.VMEM((8, 256, 512), BF16),
            pltpu.VMEM((7, room, 512), BF16),
            pltpu.VMEM((8, room, BLK), BF16),
            pltpu.VMEM((BLK, BLK), F32),
            pltpu.VMEM((256, 256), BF16),
            DMA,
            DMA((8,)),
            DMA,
            DMA((7,)),
            DMA((8,)),
            DMA((8,)),
        ],
        compiler_params=remote(number),
        name=f"forward_{room}",
    )


def backward(room, number, entries):
    return pl.pallas_call(
        functools.partial(backward_kernel, room, entries),
        out_shape=(shape((32, 32, BLK), BF16), shape((8, 128), F32)),
        in_specs=[VMEM] * 4,
        out_specs=(VMEM, VMEM),
        scratch_shapes=[
            pltpu.VMEM((2, BLK, BLK), BF16),
            pltpu.VMEM((8, room, 512), BF16),
            pltpu.VMEM((7, room, 512), BF16),
            pltpu.VMEM((8, 256, 512), BF16),
            pltpu.VMEM((256, 256), BF16),
            pltpu.VMEM((8, 512), F32),
            pltpu.VMEM((4, 8, 128), F32),
            pltpu.VMEM((16, 8, 128), F32),
            DMA((2,)),
            DMA,
            DMA((7,)),
            DMA,
            DMA,
            DMA((4,)),
            DMA((4,)),
        ],
        compiler_params=remote(number),
        name=f"backward_{room}",
    )


def body(gradients, statistics, row_counts, block_pair):
    blocks = gradients.shape[0]
    outgoing, table = pl.pallas_call(
        deal_kernel,
        out_shape=(shape(gradients.shape, BF16), shape((16, 256), jnp.int32)),
        in_specs=[SMEM, SMEM, VMEM],
        out_specs=(VMEM, VMEM),
        compiler_params=pltpu.CompilerParams(vmem_limit_bytes=16 << 20),
        name="deal",
    )(row_counts, block_pair, gradients)
    planes = jnp.sum(row_counts.reshape(4, 8, 2), axis=(0, 2))
    fits = jnp.max(planes) <= ROOM

    grad = lax.cond(fits, forward(ROOM, 0), forward(FULL, 1), outgoing, table)

    accumulated, root, step = pl.pallas_call(
        root_kernel,
        out_shape=(shape((BLK, BLK), F32), shape((BLK, BLK), BF16), shape((BLK, BLK), BF16)),
        in_specs=[VMEM, ANY],
        out_specs=(ANY, VMEM, VMEM),
        scratch_shapes=[
            pltpu.VMEM((BLK, BLK), F32),
            pltpu.VMEM((BLK, BLK), BF16),
            pltpu.VMEM((BLK, BLK), BF16),
            pltpu.VMEM((8, BLK), F32),
            pltpu.VMEM((2, BLK, BLK), BF16),
            DMA((4,)),
            DMA((4,)),
        ],
        compiler_params=pltpu.CompilerParams(vmem_limit_bytes=LIMIT),
        name="roots",
    )(grad, statistics)

    entries = lax.axis_size("mp") * blocks * BLK * BLK
    returned, scale = lax.cond(
        fits, backward(ROOM, 2, entries), backward(FULL, 3, entries), root, step, grad, table
    )

    update = pl.pallas_call(
        finish_kernel,
        out_shape=shape(gradients.shape, BF16),
        in_specs=[SMEM, VMEM, VMEM],
        out_specs=ANY,
        scratch_shapes=[pltpu.VMEM(gradients.shape, BF16), DMA((4,))],
        compiler_params=pltpu.CompilerParams(vmem_limit_bytes=16 << 20),
        name="finish",
    )(block_pair, scale, returned)
    return (update, accumulated)


def solution(mesh):
    torus = Mesh(mesh.devices.reshape(4, 8, 2, mesh.shape["mp"]), DP + ("mp",))
    placed = (P(None, DP, "mp"), P(DP, "mp"), P(), P())
    return jax.shard_map(
        body,
        mesh=torus,
        in_specs=placed,
        out_specs=(P(None, DP, "mp"), P(DP, "mp")),
        check_vma=False,
    )
```

time: 305 us -> 140 us (0.46)
  Pallas kernels: 0 us -> 131 us
  blocking collectives: 103 us -> 0 us
  other arithmetic: 57 us -> 0.76 us
  waiting for transfers between devices: 49.3 us -> 0 us
  local copies, waits for them, and re-layouts: 47.2 us -> 5.84 us
  matrix products: 35.8 us -> 0 us
  starting transfers between devices: 8.84 us -> 0 us
    pallas_call x0 -> x5, Pallas kernels: none -> 131 us  [the longest x1 57.1 us: body(): lax.cond(fits, backward(ROOM, 2, entries), backward(FULL, 3, entries), ro...]
    all_to_all x1 -> x0, blocking collectives: 64.3 us -> none  [body(): lax.all_to_all(outgoing, DP, split_axis=0, concat_axis=0, tiled=True)]
    all_to_all x1 -> x0, waiting for transfers between devices: 45.8 us -> none  [body(): lax.all_to_all(outgoing_back, DP, split_axis=0, concat_axis=0, tiled=True)]
    psum x4 -> x0, blocking collectives: 38.8 us -> none  [by_axis(): return functools.reduce(lax.psum, axes, array)]
    and x2 -> x0, other arithmetic: 36 us -> none  [the longest x1 36 us: body(): jnp.take(received.reshape(devices * slot_rows, block_size), gather_rows,...]
    dot_general x5 -> x0, matrix products: 35.8 us -> none  [the longest x1 9.66 us: body(): jnp.dot(half_prod, right_root, preferred_element_type=jnp.float32)]
    gather x12 -> x0, local copies, waits for them, and re-layouts: 29.6 us -> none  [the longest x2 10.3 us: body(): jnp.take(received.reshape(devices * slot_rows, block_size), gather_rows,...]
    unnamed x18 -> x10, local copies, waits for them, and re-layouts: 12.1 us -> 5.09 us
  transfers between devices with their start and end apart: 3 -> 0, of which waited for: 2 -> 0; matrix products, arithmetic and copies ran while one was open for 18% -> 0% of each run, Pallas kernels for 0% -> 0%
where the time goes in v2:
time: 140 us; the launch traced here: 139 us
  Pallas kernels  131 us (94%)
  local copies, waits for them, and re-layouts  5.84 us (4%)
  between operations  1.52 us (1%)
    pallas_call x1, Pallas kernels, body(): lax.cond(fits, backward(ROOM, 2, entries), backward(FULL, 3, entries), ro...  57.1 us
    pallas_call x1, Pallas kernels, body(): grad = lax.cond(fits, forward(ROOM, 0), forward(FULL, 1), outgoing, table)  55.5 us
    pallas_call x1, Pallas kernels, body(): pl.pallas_call(root_kernel, out_shape=(shape((BLK, BLK), F32), shape((BLK...  14.3 us
    unnamed x10, local copies, waits for them, and re-layouts  5.09 us
    pallas_call x1, Pallas kernels, body(): pl.pallas_call(finish_kernel, out_shape=shape(gradients.shape, BF16), in_...  3.07 us

profile of v2, /device:TPU:1, one launch (start us, length us, event | category | flops | bytes accessed | tf_op | source)
XLA Modules:
  0.0 139.3 jit_solution(9390967158875433457)
XLA Ops:
  0.6 0.8 reshape.7
  1.4 0.1 reduce_sum.9
  1.5 0.6 reduce_max.9
  2.8 0.0 copy-start.1
  2.8 1.6 %copy-done.1 = bf16[32,32,1024]{2,1,0:T(8,128)(2,1)S(1)} copy-done((bf16[32,32,1024]{2,1,0:T(8,128)(2,1)S(1)}, bf16[32,32,1024]{2,1,0:T(8,128)(2,1)}, u32[]{:S(2)}) %copy-start.1) | copy-done | bytes 2097176
  4.4 0.0 copy-start.2
  4.4 0.7 copy-done.2
  5.1 0.0 copy-start.4
  5.1 0.7 copy-done.4
  5.7 1.0 deal.1
  6.7 55.5 %conditional.2 = (bf16[1024,1024]{1,0:T(8,128)(2,1)S(1)}) conditional(s32[]{:T(128)} %convert_element_type.4, (bf16[32,32,1024]{2,1,0:T(8,128)(2,1)S(1)}, s32[16,256]{1,0:T(8,128)S(1)}) %deal.1, (bf16[32,32,1024]{2,1,0:T(8,128)(2,1)S(1)}, s32[16,256]{1,0:T(8,128)S(1)}) %deal.1), branch_computations={%region_2.0_spmd, %region_3.0_spmd} | conditional | bytes 8 | solution.py:544
  6.8 55.5 %forward_192.1 = bf16[1024,1024]{1,0:T(8,128)(2,1)S(1)} custom-call(bf16[32,32,1024]{2,1,0:T(8,128)(2,1)S(1)} %get-tuple-element.29.o_ref, s32[16,256]{1,0:T(8,128)S(1)} %get-tuple-element.30.t_ref), custom_call_target="tpu_custom_call" | custom-call | tf_op jit(solution)/shard_map/cond/branch_1_fun/forward_192/pallas_call | solution.py:544
  62.2 0.0 copy-start
  62.2 2.2 %copy-done = f32[1024,1024]{1,0:T(8,128)S(1)} copy-done((f32[1024,1024]{1,0:T(8,128)S(1)}, f32[1024,1024]{1,0:T(8,128)}, u32[]{:S(2)}) %copy-start) | copy-done | bytes 4194328
  64.4 14.3 %roots.1 = (f32[1024,1024]{1,0:T(8,128)}, bf16[1024,1024]{1,0:T(8,128)(2,1)S(1)}, bf16[1024,1024]{1,0:T(8,128)(2,1)S(1)}) custom-call(bf16[1024,1024]{1,0:T(8,128)(2,1)S(1)} %get-tuple-element.57.g_ref, f32[1024,1024]{1,0:T(8,128)S(1)} %copy-done), custom_call_target="tpu_custom_call" | custom-call | tf_op jit(solution)/shard_map/roots/pallas_call | solution.py:546
  78.7 0.0 copy-start.3
  78.7 57.3 %conditional.3 = ((bf16[32,32,1024]{2,1,0:T(8,128)(2,1)}, f32[8,128]{1,0:T(8,128)S(1)})) conditional(s32[]{:T(128)} %convert_element_type.4, (bf16[1024,1024]{1,0:T(8,128)(2,1)S(1)}, bf16[1024,1024]{1,0:T(8,128)(2,1)S(1)}, bf16[1024,1024]{1,0:T(8,128)(2,1)S(1)}, s32[16,256]{1,0:T(8,128)S(1)}) %tuple.18, (bf16[1024,1024]{1,0:T(8,128)(2,1)S(1)}, ...), branch_computations={%region_4.0_spmd, %region_5.0_spmd} | conditional | bytes 8 | solution.py:565
  78.9 57.1 %backward_192.1 = (bf16[32,32,1024]{2,1,0:T(8,128)(2,1)}, f32[8,128]{1,0:T(8,128)S(1)}) custom-call(bf16[1024,1024]{1,0:T(8,128)(2,1)S(1)} %get-tuple-element.35.root_ref, bf16[1024,1024]{1,0:T(8,128)(2,1)S(1)} %get-tuple-element.36.step_ref, bf16[1024,1024]{1,0:T(8,128)(2,1)S(1)} %get-tuple-element.37.g_ref, s32[16,256]{1,0:T(8,128)S(1)} %get-tuple-element.38.t_ref), custom_call_target="tpu_custom_call" | custom-call | tf_op jit(solution)/shard_map/cond/branch_1_fun/backward_192/pallas_call | solution.py:565
  136.0 0.0 copy-done.3
  136.1 3.1 %finish.1 = bf16[32,32,1024]{2,1,0:T(8,128)(2,1)} custom-call(s32[32]{0:T(128)S(1)} %copy-done.3, f32[8,128]{1,0:T(8,128)S(1)} %get-tuple-element.50.scale_ref, bf16[32,32,1024]{2,1,0:T(8,128)(2,1)} %get-tuple-element.51.f_ref), custom_call_target="tpu_custom_call" | custom-call | tf_op jit(solution)/shard_map/finish/pallas_call | solution.py:569
Async XLA Ops:
  2.8 1.6 %copy-start.1 = (bf16[32,32,1024]{2,1,0:T(8,128)(2,1)S(1)}, bf16[32,32,1024]{2,1,0:T(8,128)(2,1)}, u32[]{:S(2)}) copy-start(bf16[32,32,1024]{2,1,0:T(8,128)(2,1)} %g_ref.1) | copy-start | bytes 6291460
  4.4 0.7 copy-start.2
  5.1 0.7 copy-start.4
  62.2 2.2 %copy-start = (f32[1024,1024]{1,0:T(8,128)S(1)}, f32[1024,1024]{1,0:T(8,128)}, u32[]{:S(2)}) copy-start(f32[1024,1024]{1,0:T(8,128)} %s_ref.1) | copy-start | bytes 12582916
  78.7 57.3 %copy-start.3 = (s32[32]{0:T(128)S(1)}, s32[32]{0:T(128)}, u32[]{:S(2)}) copy-start(s32[32]{0:T(128)} %pair.3) | copy-start | bytes 388

commit v3 on v2

v3 whole, which is shorter than its diff:
```python
import functools

import jax
import jax.numpy as jnp
from jax import lax
from jax.experimental import pallas as pl
from jax.experimental.pallas import tpu as pltpu
from jax.sharding import Mesh
from jax.sharding import PartitionSpec as P

DP = ("dp_0", "dp_1", "dp_2")
BLK = 1024
TILE = 256
F32 = jnp.float32
BF16 = jnp.bfloat16

decay_rate = 0.95
epsilon = 1e-06


def place():
    return (
        lax.axis_index("dp_0"),
        lax.axis_index("dp_1"),
        lax.axis_index("dp_2"),
        lax.axis_index("mp"),
    )


def distance(step):
    odd = step % 2
    return (4 + odd * ((step + 1) // 2) - (1 - odd) * (step // 2)) % 8


def dot(a, b, dims=((1,), (0,))):
    return lax.dot_general(a, b, (dims, ((), ())), preferred_element_type=F32)


def greet(peers):
    barrier = pltpu.get_barrier_semaphore()
    for peer in peers:
        pl.semaphore_signal(barrier, inc=1, device_id=peer)
    return barrier, len(peers)


def plane_peers(x, c):
    return [
        {"dp_0": (x + dx) % 4, "dp_2": (c + dc) % 2}
        for dx in range(4)
        for dc in range(2)
        if dx or dc
    ]


def z_peers(z):
    return [{"dp_1": (z + dz) % 8} for dz in range(1, 8)]


def transfer(ref, send_sem, recv_sem, c):
    return pltpu.make_async_remote_copy(
        ref, ref, send_sem, recv_sem, device_id={"dp_2": (c + 1) % 2}
    )


def half_of(c):
    return pl.ds(pl.multiple_of(512 * c, 512), 512)


def slots_of(x, c):
    return pl.ds(pl.multiple_of(32 * (2 * x + c), 32), 32)


def span(tile):
    return pl.ds(pl.multiple_of(tile * TILE, TILE), TILE)


def deal_kernel(
    counts_ref, pair_ref, g_ref, o_ref, t_ref, level_ref, counts, pair, sem, block_sem
):
    first = pltpu.make_async_copy(pair_ref, pair, sem.at[0])
    second = pltpu.make_async_copy(counts_ref, counts, sem.at[1])
    first.start()
    second.start()
    first.wait()

    @pl.loop(0, 32)
    def _(k):
        pltpu.make_async_copy(g_ref.at[k], o_ref.at[pair[k]], block_sem).start()

    second.wait()
    lane = lax.broadcasted_iota(jnp.int32, (8, 256), 1)
    plane = lax.broadcasted_iota(jnp.int32, (8, 256), 0)
    inner = lane % 32
    group = lane // 32
    spot = jnp.full((8, 256), -1, jnp.int32)
    target = jnp.full((8, 256), -1, jnp.int32)
    offset = counts[0] * 0
    filled = [offset] * 8
    for x in range(4):
        for z in range(8):
            for c in range(2):
                q = (x * 8 + z) * 2 + c
                n = counts[q]
                at = filled[z]
                here = (plane == z) & (group == 2 * x + c) & (inner < n)
                spot = jnp.where(here, at + inner, spot)
                held = (plane == z) & (lane >= at) & (lane < at + n)
                target = jnp.where(held, offset - at + lane, target)
                filled[z] = at + n
                offset = offset + n
    t_ref[0:8, :] = spot
    t_ref[8:16, :] = target
    most = filled[0]
    for z in range(1, 8):
        most = jnp.maximum(most, filled[z])
    level = jnp.int32(0)
    for room in ROOMS[:-1]:
        level = level + jnp.where(most > room, 1, 0)
    level_ref[0] = level
    pltpu.make_async_copy(g_ref, o_ref, block_sem).wait()


def step_kernel(
    room,
    entries,
    o_ref,
    t_ref,
    s_ref,
    f_ref,
    scale_ref,
    a_out,
    near,
    packed,
    recv,
    acc,
    pick_ref,
    picks,
    grad,
    a,
    poly,
    root,
    moment,
    work,
    fourth,
    roots,
    ways,
    back,
    slots,
    spread_ref,
    square,
    told,
    heard,
    x_send,
    x_recv,
    z_send,
    z_recv,
    p_send,
    p_recv,
    in_sem,
    out_sem,
    root_sem,
    bz_send,
    bz_recv,
    bx_send,
    bx_recv,
    sum_send,
    sum_recv,
    loc_sem,
):
    x, z, c, y = place()
    partner = {"dp_2": (c + 1) % 2}
    y_peers = [{"mp": (y + dy) % 4} for dy in range(1, 4)]
    x_peers = [{"dp_0": (x + dx) % 4} for dx in range(1, 4)]
    barrier, count = greet(plane_peers(x, c) + z_peers(z) + y_peers)
    tiles = BLK // TILE

    def fetch(tile):
        return pltpu.make_async_copy(s_ref.at[span(tile), :], a.at[span(tile), :], in_sem.at[tile])

    def flush(tile):
        return pltpu.make_async_copy(a.at[span(tile), :], a_out.at[span(tile), :], out_sem.at[tile])

    for tile in range(tiles):
        fetch(tile).start()

    rows = lax.broadcasted_iota(jnp.int32, (256, 256), 0)
    pick_ref[...] = jnp.where(rows == t_ref[pl.ds(z, 1), :], 1.0, 0.0).astype(BF16)

    def column(line):
        turned = jnp.transpose(jnp.broadcast_to(line.astype(F32), (128, 256)))
        return jnp.concatenate([turned] * 8, axis=1)

    cols = lax.broadcasted_iota(jnp.int32, (256, BLK), 1).astype(F32)
    spread = jnp.where(column(t_ref[pl.ds(z, 1), :]) == cols, 1.0, 0.0)
    spread_ref[...] = spread[:, 0:256].astype(BF16)
    square[...] = jnp.zeros_like(square)
    pl.semaphore_wait(barrier, count)

    @pl.loop(0, 8)
    def _(step):
        tz = (z + distance(step)) % 8
        for dx in range(4):
            for dc in range(2):
                tx, tc = (x + dx) % 4, (c + dc) % 2
                if dx or dc:
                    pltpu.make_async_remote_copy(
                        o_ref.at[tx * 8 + tz, :, half_of(tc)],
                        near.at[step, slots_of(x, c), :],
                        x_send,
                        x_recv.at[step],
                        device_id={"dp_0": tx, "dp_2": tc},
                    ).start()

    @pl.loop(0, 8)
    def _(step):
        tz = (z + distance(step)) % 8
        near[step, slots_of(x, c), :] = o_ref[x * 8 + tz, :, half_of(c)]

    def pack(step):
        transfer(near.at[step, pl.ds(0, 224), :], x_send, x_recv.at[step], c).wait_recv()
        return dot(pick_ref[pl.ds(0, room), :], near[step]).astype(BF16)

    def to_partner(step):
        part = recv.at[step, :, half_of(c)]
        return pltpu.make_async_remote_copy(
            part, part, p_send.at[step], p_recv.at[step], device_id=partner
        )

    @pl.loop(0, 7)
    def _(step):
        packed[step] = pack(step)
        pltpu.make_async_remote_copy(
            packed.at[step],
            recv.at[step, :, half_of(c)],
            z_send,
            z_recv.at[step],
            device_id={"dp_1": (z + distance(step)) % 8},
        ).start()

    recv[7, :, half_of(c)] = pack(7)
    to_partner(7).start()

    @pl.loop(0, 8)
    def _(step):
        zt = (z + distance(step)) % 8
        want = column(t_ref[pl.ds(8 + zt, 1), :]) == cols
        picks[step] = jnp.where(want, 1.0, 0.0).astype(BF16)[0:room, :]

    lines = lax.broadcasted_iota(jnp.int32, (TILE, room), 0)

    def put(step, first=False, last=False):
        to_partner(step).wait_recv()
        zs = (z + 8 - distance(step)) % 8
        target = t_ref[pl.ds(8 + zs, 1), :][:, 0:room]

        @pl.loop(0, tiles)
        def _(tile):
            pick = jnp.where(lines + tile * TILE == target, 1.0, 0.0).astype(BF16)
            new = dot(pick, recv[step])
            if not first:
                new = acc[span(tile), :] + new
            if last:
                grad[span(tile), :] = new.astype(BF16)
            else:
                acc[span(tile), :] = new

    def take(step):
        transfer(packed.at[step], z_send, z_recv.at[step], c).wait_recv()
        to_partner(step).start()

    take(0)
    put(7, first=True)

    @pl.loop(1, 7)
    def _(step):
        take(step)
        put(step - 1)

    put(6, last=True)

    def gram(side):
        def add(tile, total):
            if side == 0:
                prod = dot(grad[span(tile), :], grad[...], ((1,), (1,)))
            else:
                prod = dot(grad[:, span(tile)], grad[...], ((0,), (0,)))
            new = decay_rate * a[span(tile), :] + (1.0 - decay_rate) * prod
            a[span(tile), :] = new
            return total + jnp.sum(jnp.abs(new).reshape(TILE // 8, 8, BLK), axis=0)

        work[...] = lax.fori_loop(0, tiles, add, jnp.zeros((8, BLK), F32))

    for tile in range(tiles):
        fetch(tile).wait()
    pl.when(c == 0)(lambda: gram(0))
    pl.when(c == 1)(lambda: gram(1))
    bound = jnp.max(jnp.sum(work[...], axis=0, keepdims=True), axis=1, keepdims=True)
    scale = 1.0 / bound
    factor = lax.rsqrt(jnp.sqrt(bound))
    row = lax.broadcasted_iota(jnp.int32, (TILE, BLK), 0)
    col = lax.broadcasted_iota(jnp.int32, (TILE, BLK), 1)

    def eye5(tile):
        return jnp.where(row + tile * TILE == col, 5.0, 0.0)

    @pl.loop(0, tiles)
    def _(tile):
        first = a[span(tile), :] * scale
        shifted = (eye5(tile) - first) * 0.25
        moment[span(tile), :] = first.astype(BF16)
        poly[span(tile), :] = shifted.astype(BF16)
        root[span(tile), :] = (factor * shifted).astype(BF16)

    for tile in range(tiles):
        flush(tile).start()

    @pl.loop(0, tiles)
    def _(tile):
        fourth[0, span(tile), :] = dot(poly[span(tile), :], poly[...]).astype(BF16)

    @pl.loop(0, tiles)
    def _(tile):
        fourth[1, span(tile), :] = dot(fourth[0, span(tile), :], fourth[0]).astype(BF16)

    @pl.loop(0, tiles)
    def _(tile):
        new = dot(fourth[1, span(tile), :], moment[...])
        poly[span(tile), :] = ((eye5(tile) - new) * 0.25).astype(BF16)

    @pl.loop(0, tiles)
    def _(tile):
        roots[c, span(tile), :] = dot(root[span(tile), :], poly[...]).astype(BF16)
        part = roots.at[c, span(tile), :]
        pltpu.make_async_remote_copy(
            part, part, root_sem.at[0], root_sem.at[1], device_id=partner
        ).start()

    whole = transfer(roots.at[c], root_sem.at[0], root_sem.at[1], c)
    whole.wait_recv()

    def make(step):
        picked = dot(picks[step], roots[0]).astype(BF16)
        half = dot(picked, grad[...]).astype(BF16)
        full = dot(half, roots[1, :, half_of(c)])
        ways[step] = full.astype(BF16)
        square[...] += jnp.sum((full * full).reshape(room // 8, 8, 512), axis=0)

    @pl.loop(0, 7)
    def _(step):
        make(step)
        pltpu.make_async_remote_copy(
            ways.at[step],
            back.at[step],
            bz_send,
            bz_recv.at[step],
            device_id={"dp_1": (z + distance(step)) % 8},
        ).start()

    make(7)
    one = pl.ds(0, 1)

    def tell(stage, part, peers, at):
        told[stage, one, :] = part
        for i, peer in enumerate(peers):
            pltpu.make_async_remote_copy(
                told.at[stage, one, :],
                heard.at[at + i, one, :],
                sum_send.at[stage],
                sum_recv.at[stage],
                device_id=peer,
            ).start()

    def hear(stage, part, number, at):
        ref = heard.at[pl.ds(at, number), one, :]
        transfer(ref, sum_send.at[stage], sum_recv.at[stage], c).wait()
        for i in range(number):
            part = part + heard[at + i, one, :]
        return part

    def give(step, lot):
        slots[step] = dot(spread_ref[:, 0:room], lot).astype(BF16)
        block = x * 8 + (z + 8 - distance(step)) % 8
        for dx in range(4):
            for dc in range(2):
                tx, tc = (x + dx) % 4, (c + dc) % 2
                if dx or dc:
                    pltpu.make_async_remote_copy(
                        slots.at[step, slots_of(tx, tc), :],
                        f_ref.at[block, :, half_of(c)],
                        bx_send,
                        bx_recv,
                        device_id={"dp_0": tx, "dp_2": tc},
                    ).start()
        pltpu.make_async_copy(
            slots.at[step, slots_of(x, c), :], f_ref.at[block, :, half_of(c)], loc_sem
        ).start()

    def pass_on(step):
        transfer(back.at[step], bz_send, bz_recv.at[step], c).wait_recv()
        give(step, back[step])

    own = jnp.sum(square[...], axis=0, keepdims=True)
    part = own[:, 0:128] + own[:, 128:256] + own[:, 256:384] + own[:, 384:512]
    tell(0, part, [partner], 0)
    give(7, ways[7])
    part = hear(0, part, 1, 0)
    tell(1, part, y_peers, 1)
    pass_on(0)
    part = hear(1, part, 3, 1)
    tell(2, part, x_peers, 4)
    pass_on(1)
    part = hear(2, part, 3, 4)
    tell(3, part, z_peers(z), 7)

    @pl.loop(2, 7)
    def _(step):
        pass_on(step)

    part = hear(3, part, 7, 7)
    mean = jnp.sum(part, axis=1, keepdims=True) * (1.0 / entries)
    scale_ref[...] = jnp.broadcast_to(lax.rsqrt(mean + epsilon), (8, 128))

    @pl.loop(0, 8)
    def _(step):
        to_partner(step).wait_send()

    transfer(near.at[pl.ds(0, 7)], x_send, x_recv.at[0], c).wait_send()
    transfer(packed, z_send, z_recv.at[0], c).wait_send()
    whole.wait_send()
    for tile in range(tiles):
        flush(tile).wait()
    transfer(ways.at[pl.ds(0, 7)], bz_send, bz_recv.at[0], c).wait_send()
    transfer(slots.at[pl.ds(0, 7)], bx_send, bx_recv, c).wait_send()
    pltpu.make_async_copy(slots.at[0], slots.at[0], loc_sem).wait()
    transfer(f_ref.at[pl.ds(0, 28)], bx_send, bx_recv, c).wait_recv()


def finish_kernel(
    pair_ref, scale_ref, f_ref, a_ref, u_ref, a_out, pair, block, held, a, sem, in_sem, out_sem, u_sem
):
    first = pltpu.make_async_copy(pair_ref, pair, sem.at[0])
    second = pltpu.make_async_copy(f_ref, block, sem.at[1])
    first.start()
    second.start()

    def fetch(tile):
        return pltpu.make_async_copy(a_ref.at[span(tile), :], a.at[span(tile), :], in_sem.at[tile])

    def store(tile):
        return pltpu.make_async_copy(a.at[span(tile), :], a_out.at[span(tile), :], out_sem.at[tile])

    def flush(group):
        part = pl.ds(group * 8, 8)
        return pltpu.make_async_copy(held.at[part], u_ref.at[part], u_sem.at[group])

    for tile in range(4):
        fetch(tile).start()
    scale = scale_ref[0:1, 0:1]
    first.wait()
    second.wait()

    @pl.loop(0, 4)
    def _(group):
        for i in range(8):
            k = group * 8 + i
            held[k] = (block[pair[k]].astype(F32) * scale).astype(BF16)
        flush(group).start()
        fetch(group).wait()
        store(group).start()

    for group in range(4):
        flush(group).wait()
        store(group).wait()


VMEM = pl.BlockSpec(memory_space=pltpu.VMEM)
SMEM = pl.BlockSpec(memory_space=pltpu.SMEM)
HBM = pl.BlockSpec(memory_space=pltpu.HBM)
DMA = pltpu.SemaphoreType.DMA
ROOMS = (176, 192, 208, 256)


def shape(dims, kind):
    return jax.ShapeDtypeStruct(dims, kind)


def step_call(room, number, entries):
    return pl.pallas_call(
        functools.partial(step_kernel, room, entries),
        out_shape=(
            shape((32, 32, BLK), BF16),
            shape((8, 128), F32),
            shape((BLK, BLK), F32),
        ),
        in_specs=[VMEM, VMEM, HBM],
        out_specs=(HBM, VMEM, HBM),
        scratch_shapes=[
            pltpu.VMEM((8, 256, 512), BF16),
            pltpu.VMEM((7, room, 512), BF16),
            pltpu.VMEM((8, room, BLK), BF16),
            pltpu.VMEM((BLK, BLK), F32),
            pltpu.VMEM((256, 256), BF16),
            pltpu.VMEM((8, room, BLK), BF16),
            pltpu.VMEM((BLK, BLK), BF16),
            pltpu.VMEM((BLK, BLK), F32),
            pltpu.VMEM((BLK, BLK), BF16),
            pltpu.VMEM((BLK, BLK), BF16),
            pltpu.VMEM((BLK, BLK), BF16),
            pltpu.VMEM((8, BLK), F32),
            pltpu.VMEM((2, BLK, BLK), BF16),
            pltpu.VMEM((2, BLK, BLK), BF16),
            pltpu.VMEM((8, room, 512), BF16),
            pltpu.VMEM((7, room, 512), BF16),
            pltpu.VMEM((8, 256, 512), BF16),
            pltpu.VMEM((256, 256), BF16),
            pltpu.VMEM((8, 512), F32),
            pltpu.VMEM((4, 8, 128), F32),
            pltpu.VMEM((16, 8, 128), F32),
            DMA,
            DMA((8,)),
            DMA,
            DMA((7,)),
            DMA((8,)),
            DMA((8,)),
            DMA((4,)),
            DMA((4,)),
            DMA((2,)),
            DMA,
            DMA((7,)),
            DMA,
            DMA,
            DMA((4,)),
            DMA((4,)),
            DMA,
        ],
        compiler_params=pltpu.CompilerParams(
            collective_id=number, has_side_effects=True, vmem_limit_bytes=56 << 20
        ),
        name=f"step_{room}",
    )


def body(gradients, statistics, row_counts, block_pair):
    blocks = gradients.shape[0]
    outgoing, table, level = pl.pallas_call(
        deal_kernel,
        out_shape=(
            shape(gradients.shape, BF16),
            shape((16, 256), jnp.int32),
            shape((1,), jnp.int32),
        ),
        in_specs=[HBM, HBM, HBM],
        out_specs=(VMEM, VMEM, SMEM),
        scratch_shapes=[
            pltpu.SMEM((64,), jnp.int32),
            pltpu.SMEM((32,), jnp.int32),
            DMA((2,)),
            DMA,
        ],
        compiler_params=pltpu.CompilerParams(vmem_limit_bytes=64900000),
        name="deal",
    )(row_counts, block_pair, gradients)

    entries = lax.axis_size("mp") * blocks * BLK * BLK
    returned, scale, accumulated = lax.switch(
        level[0],
        [step_call(room, i, entries) for i, room in enumerate(ROOMS)],
        outgoing,
        table,
        statistics,
    )

    return pl.pallas_call(
        finish_kernel,
        out_shape=(shape(gradients.shape, BF16), shape((BLK, BLK), F32)),
        in_specs=[HBM, VMEM, HBM, HBM],
        out_specs=(HBM, HBM),
        scratch_shapes=[
            pltpu.SMEM((32,), jnp.int32),
            pltpu.VMEM(gradients.shape, BF16),
            pltpu.VMEM(gradients.shape, BF16),
            pltpu.VMEM((BLK, BLK), F32),
            DMA((2,)),
            DMA((4,)),
            DMA((4,)),
            DMA((4,)),
        ],
        compiler_params=pltpu.CompilerParams(vmem_limit_bytes=24 << 20),
        name="finish",
    )(block_pair, scale, returned, accumulated)


def solution(mesh):
    torus = Mesh(mesh.devices.reshape(4, 8, 2, mesh.shape["mp"]), DP + ("mp",))
    placed = (P(None, DP, "mp"), P(DP, "mp"), P(), P())
    return jax.shard_map(
        body,
        mesh=torus,
        in_specs=placed,
        out_specs=(P(None, DP, "mp"), P(DP, "mp")),
        check_vma=False,
    )
```

time: 140 us -> 127 us (0.907)
  Pallas kernels: 131 us -> 125 us
  local copies, waits for them, and re-layouts: 5.84 us -> 0.01 us
    pallas_call x4 -> x2, Pallas kernels: 130 us -> 122 us  [the longest x1 117 us: body(): lax.switch(level[0], [step_call(room, i, entries) for i, room in enumerat...]
    unnamed x10 -> x2, local copies, waits for them, and re-layouts: 5.09 us -> 0.01 us
    pallas_call x1, Pallas kernels: 1.02 us -> 2.79 us  [body(): pl.pallas_call(deal_kernel, out_shape=(shape(gradients.shape, BF16), shap...]
where the time goes in v3:
time: 127 us
  Pallas kernels  125 us (98%)
  between operations  1.53 us (1%)
    pallas_call x1, Pallas kernels, body(): lax.switch(level[0], [step_call(room, i, entries) for i, room in enumerat...  117 us
    pallas_call x1, Pallas kernels, body(): pl.pallas_call(finish_kernel, out_shape=(shape(gradients.shape, BF16), sh...  5.47 us
    pallas_call x1, Pallas kernels, body(): pl.pallas_call(deal_kernel, out_shape=(shape(gradients.shape, BF16), shap...  2.79 us

profile of v3, /device:TPU:1, one launch (start us, length us, event | category | flops | bytes accessed | tf_op | source)
XLA Modules:
  0.0 127.2 jit_solution(10855810194409581493)
XLA Ops:
  0.6 2.8 %deal.1 = (bf16[32,32,1024]{2,1,0:T(8,128)(2,1)S(1)}, s32[16,256]{1,0:T(8,128)S(1)}, s32[1]{0:T(128)}) custom-call(s32[64]{0:T(128)} %counts_ref.1, s32[32]{0:T(128)} %pair_ref.3, bf16[32,32,1024]{2,1,0:T(8,128)(2,1)} %g_ref.1), custom_call_target="tpu_custom_call" | custom-call | tf_op jit(solution)/shard_map/deal/pallas_call | solution.py:545
  4.1 0.0 copy-start
  4.1 117.4 %conditional.1 = ((bf16[32,32,1024]{2,1,0:T(8,128)(2,1)}, f32[8,128]{1,0:T(8,128)S(1)}, f32[1024,1024]{1,0:T(8,128)})) conditional(s32[]{:T(128)} %bitcast, (bf16[32,32,1024]{2,1,0:T(8,128)(2,1)S(1)}, s32[16,256]{1,0:T(8,128)S(1)}, f32[1024,1024]{1,0:T(8,128)}) %tuple.19, (bf16[32,32,1024]{2,1,0:T(8,128)(2,1)S(1)}, ...), branch_computations={%region_0.0_spmd, %region_1.0_spmd, %region_2.0_spmd, %region_3.0_... | conditional | bytes 8 | solution.py:565
  4.1 116.9 %step_176.1 = (bf16[32,32,1024]{2,1,0:T(8,128)(2,1)}, f32[8,128]{1,0:T(8,128)S(1)}, f32[1024,1024]{1,0:T(8,128)}) custom-call(bf16[32,32,1024]{2,1,0:T(8,128)(2,1)S(1)} %get-tuple-element.24.o_ref, s32[16,256]{1,0:T(8,128)S(1)} %get-tuple-element.25.t_ref, f32[1024,1024]{1,0:T(8,128)} %get-tuple-element.26.s_ref), custom_call_target="tpu_custom_call" | custom-call | tf_op jit(solution)/shard_map/cond/branch_0_fun/step_176/pallas_call | solution.py:565
  121.5 0.0 copy-done
  121.6 5.5 %finish.1 = (bf16[32,32,1024]{2,1,0:T(8,128)(2,1)}, f32[1024,1024]{1,0:T(8,128)}) custom-call(s32[32]{0:T(128)S(1)} %copy-done, f32[8,128]{1,0:T(8,128)S(1)} %get-tuple-element.47.scale_ref, bf16[32,32,1024]{2,1,0:T(8,128)(2,1)} %get-tuple-element.48.f_ref, f32[1024,1024]{1,0:T(8,128)} %get-tuple-element.49.a_ref), custom_call_target="tpu_custom_call" | custom-call | tf_op jit(solution)/shard_map/finish/pallas_call | solution.py:573
Async XLA Ops:
  4.1 117.5 %copy-start = (s32[32]{0:T(128)S(1)}, s32[32]{0:T(128)}, u32[]{:S(2)}) copy-start(s32[32]{0:T(128)} %pair_ref.3) | copy-start | bytes 388

commit v4 on v3

--- a/solution.py
+++ b/solution.py
@@ -30,6 +30,13 @@
 def distance(step):
     odd = step % 2
     return (4 + odd * ((step + 1) // 2) - (1 - odd) * (step // 2)) % 8
+
+
+def outward(step):
+    if isinstance(step, int) and step == 7:
+        return 0
+    odd = step % 2
+    return (1 - odd) * (1 + step // 2) + odd * (7 - step // 2)
 
 
 def dot(a, b, dims=((1,), (0,))):
@@ -226,6 +233,13 @@
             part, part, p_send.at[step], p_recv.at[step], device_id=partner
         )
 
+    def choose(step):
+        zt = (z + outward(step)) % 8
+        want = column(t_ref[pl.ds(8 + zt, 1), :]) == cols
+        picks[step] = jnp.where(want, 1.0, 0.0).astype(BF16)[0:room, :]
+
+    choose(7)
+
     @pl.loop(0, 7)
     def _(step):
         packed[step] = pack(step)
@@ -236,15 +250,10 @@
             z_recv.at[step],
             device_id={"dp_1": (z + distance(step)) % 8},
         ).start()
+        choose(step)
 
     recv[7, :, half_of(c)] = pack(7)
     to_partner(7).start()
-
-    @pl.loop(0, 8)
-    def _(step):
-        zt = (z + distance(step)) % 8
-        want = column(t_ref[pl.ds(8 + zt, 1), :]) == cols
-        picks[step] = jnp.where(want, 1.0, 0.0).astype(BF16)[0:room, :]
 
     lines = lax.broadcasted_iota(jnp.int32, (TILE, room), 0)
 
@@ -353,7 +362,7 @@
             back.at[step],
             bz_send,
             bz_recv.at[step],
-            device_id={"dp_1": (z + distance(step)) % 8},
+            device_id={"dp_1": (z + outward(step)) % 8},
         ).start()
 
     make(7)
@@ -379,7 +388,7 @@
 
     def give(step, lot):
         slots[step] = dot(spread_ref[:, 0:room], lot).astype(BF16)
-        block = x * 8 + (z + 8 - distance(step)) % 8
+        block = x * 8 + (z + 8 - outward(step)) % 8
         for dx in range(4):
             for dc in range(2):
                 tx, tc = (x + dx) % 4, (c + dc) % 2

time: 127 us -> 126 us (level)
  the two profiles are of different devices: /device:TPU:1 before, /device:TPU:81 now
where the time goes in v4:
time: 126 us
  Pallas kernels  124 us (98%)
  between operations  1.53 us (1%)
    pallas_call x1, Pallas kernels, body(): lax.switch(level[0], [step_call(room, i, entries) for i, room in enumerat...  116 us
    pallas_call x1, Pallas kernels, body(): pl.pallas_call(finish_kernel, out_shape=(shape(gradients.shape, BF16), sh...  5.47 us
    pallas_call x1, Pallas kernels, body(): pl.pallas_call(deal_kernel, out_shape=(shape(gradients.shape, BF16), shap...  2.79 us

profile of v4, /device:TPU:81, one launch (start us, length us, event | category | flops | bytes accessed | tf_op | source)
XLA Modules:
  0.0 125.9 jit_solution(3293159071950681080)
XLA Ops:
  0.6 2.8 %deal.1 = (bf16[32,32,1024]{2,1,0:T(8,128)(2,1)S(1)}, s32[16,256]{1,0:T(8,128)S(1)}, s32[1]{0:T(128)}) custom-call(s32[64]{0:T(128)} %counts_ref.1, s32[32]{0:T(128)} %pair_ref.3, bf16[32,32,1024]{2,1,0:T(8,128)(2,1)} %g_ref.1), custom_call_target="tpu_custom_call" | custom-call | tf_op jit(solution)/shard_map/deal/pallas_call | solution.py:554
  4.1 0.0 copy-start
  4.1 116.1 %conditional.1 = ((bf16[32,32,1024]{2,1,0:T(8,128)(2,1)}, f32[8,128]{1,0:T(8,128)S(1)}, f32[1024,1024]{1,0:T(8,128)})) conditional(s32[]{:T(128)} %bitcast, (bf16[32,32,1024]{2,1,0:T(8,128)(2,1)S(1)}, s32[16,256]{1,0:T(8,128)S(1)}, f32[1024,1024]{1,0:T(8,128)}) %tuple.19, (bf16[32,32,1024]{2,1,0:T(8,128)(2,1)S(1)}, ...), branch_computations={%region_0.0_spmd, %region_1.0_spmd, %region_2.0_spmd, %region_3.0_... | conditional | bytes 8 | solution.py:574
  4.1 115.6 %step_176.1 = (bf16[32,32,1024]{2,1,0:T(8,128)(2,1)}, f32[8,128]{1,0:T(8,128)S(1)}, f32[1024,1024]{1,0:T(8,128)}) custom-call(bf16[32,32,1024]{2,1,0:T(8,128)(2,1)S(1)} %get-tuple-element.24.o_ref, s32[16,256]{1,0:T(8,128)S(1)} %get-tuple-element.25.t_ref, f32[1024,1024]{1,0:T(8,128)} %get-tuple-element.26.s_ref), custom_call_target="tpu_custom_call" | custom-call | tf_op jit(solution)/shard_map/cond/branch_0_fun/step_176/pallas_call | solution.py:574
  120.2 0.0 copy-done
  120.2 5.5 %finish.1 = (bf16[32,32,1024]{2,1,0:T(8,128)(2,1)}, f32[1024,1024]{1,0:T(8,128)}) custom-call(s32[32]{0:T(128)S(1)} %copy-done, f32[8,128]{1,0:T(8,128)S(1)} %get-tuple-element.47.scale_ref, bf16[32,32,1024]{2,1,0:T(8,128)(2,1)} %get-tuple-element.48.f_ref, f32[1024,1024]{1,0:T(8,128)} %get-tuple-element.49.a_ref), custom_call_target="tpu_custom_call" | custom-call | tf_op jit(solution)/shard_map/finish/pallas_call | solution.py:582
Async XLA Ops:
  4.1 116.2 %copy-start = (s32[32]{0:T(128)S(1)}, s32[32]{0:T(128)}, u32[]{:S(2)}) copy-start(s32[32]{0:T(128)} %pair_ref.3) | copy-start | bytes 388
